TPU v7x, 512 devices: a 8x2x16 block of a 8x8x16 slice. The times are simulated.
512 devices in a mesh: rep: 2 (over y), seq: 16 (over z), head: 8 (over x), sub: 2 (over core).
Axes of the slice: x: 8, y: 2, z: 16, core: 2. Of those that a mesh axis runs over, the one named last changes fastest.
The devices are a block of a 8x8x16 slice.
Arguments:
- queries: bfloat16 [32, 8192], P('rep', 'head'), parts along dimension 0, may hold values from -4.5 to 4.5
- key_cache: bfloat16 [4096, 128, 1024], P(('rep', 'seq', 'sub'), None, 'head'), parts along dimension 0, may hold values from -4.5 to 4.5
- value_cache: bfloat16 [4096, 128, 1024], P(('rep', 'seq', 'sub'), None, 'head'), parts along dimension 0, may hold values from -6 to 6
- seq_lengths: int32 [32], P('rep'), parts along dimension 0, may hold values from 513 to 32768, as said below
- slot_owner: int32 [4096], P(('rep', 'seq', 'sub')), parts along dimension 0, may hold values from 0 to 15, as said below
- slot_page: int32 [4096], P(('rep', 'seq', 'sub')), parts along dimension 0, may hold values from 0 to 255, as said below
- out_weight: bfloat16 [8192, 8192], P('head', ('seq', 'sub')), may hold values from -0.0625 to 0.0625
Outputs:
- projected: bfloat16 [32, 8192], P('rep', ('seq', 'sub')), parts along dimension 0
There are 2 independent parts, one for each index of `rep`. A program takes and returns all parts, laid end to end along the dimension named above; an argument that names none is the same for every part. Nothing has to cross between parts.
Inputs may be any that keep to these rules, and one draw needn't show every extreme that they name: `slot_owner`: every sequence holds 5 to 256 pages, and some sequence exactly 256; its pages are numbered 0 upward and each stands in exactly one cache page; every cache page is used; a sequence's pages occupy consecutive cache pages. slot_page[s] < ceil(seq_lengths[slot_owner[s]] / 128), and every page below that count is present. seq_lengths[b] lies in the last of its sequence's pages.
All inputs are finite; a program needn't handle non-finite values.
Results may differ from a plain program's by a relative error of at most 0.0055.
Values may be sent and summed in bfloat16 or wider, within the bound.
A program may use at most 64 MiB of HBM per device.

v0:
```python
import jax
import jax.numpy as jnp
from jax import lax
from jax.sharding import PartitionSpec as P

DH = 128
PAGE = 128


neg_fill = -1e30


def copy_for_each(shard, axis):
    size = lax.axis_size(axis)
    return lax.all_to_all(
        jnp.broadcast_to(shard[None], (size, *shard.shape)), axis, 0, 0, tiled=True
    )


def over_copies(shard, axis):
    everything = copy_for_each(shard, axis)
    return jnp.max(everything, axis=0)


def taken_together(shard, axis):
    everything = copy_for_each(shard, axis)
    return jnp.sum(everything, axis=0)


def split_up(shard, dim, size):
    shape = shard.shape
    blocks = shard.reshape(*shape[:dim], size, shape[dim] // size, *shape[dim + 1 :])
    return jnp.moveaxis(blocks, dim, 0)


def sum_at_owner(shard, axis, dim):
    blocks = split_up(shard, dim, lax.axis_size(axis))
    arrived = lax.all_to_all(blocks, axis, split_axis=0, concat_axis=0, tiled=True)
    return arrived.sum(axis=0)


def joined_along(blocks, dim):
    blocks = jnp.moveaxis(blocks, 0, dim)
    shape = blocks.shape
    return blocks.reshape(*shape[:dim], shape[dim] * shape[dim + 1], *shape[dim + 2 :])


def gathered_copies(shard, axis, dim):
    blocks = copy_for_each(shard, axis)
    return joined_along(blocks, dim)


def spread(values, factor):
    row_count, col_count = factor.shape
    return (values.reshape(row_count, col_count, -1) * factor[:, :, None]).reshape(row_count, -1)


def on_device(queries, key_cache, value_cache, seq_lengths, slot_owner, slot_page, out_weight):
    batch_rows = queries.shape[0]
    slot_count = key_cache.shape[0]
    groups_local = key_cache.shape[2] // DH
    per_group = queries.shape[1] // (groups_local * DH)
    picked = jnp.take(queries, slot_owner, axis=0).reshape(slot_count, groups_local, per_group, DH)
    key_tiles = key_cache.reshape(slot_count, PAGE, groups_local, DH)
    value_tiles = value_cache.reshape(slot_count, PAGE, groups_local, DH)
    scores = jnp.einsum("sgjd,stgd->sgjt", picked, key_tiles, preferred_element_type=jnp.float32)
    scores = scores * (1.0 / jnp.sqrt(jnp.float32(DH)))
    valid = jnp.clip(jnp.take(seq_lengths, slot_owner, axis=0) - slot_page * PAGE, 0, PAGE)
    positions = jnp.arange(PAGE, dtype=jnp.int32)
    live = (positions[None, :] < valid[:, None])[:, None, None, :]
    scores = jnp.where(live, scores, neg_fill)
    page_peak = jnp.max(scores, axis=-1)
    probs = jnp.exp(scores - page_peak[..., None]).astype(jnp.bfloat16)
    page_mass = jnp.sum(probs.astype(jnp.float32), axis=-1)
    page_out = jnp.einsum("sgjt,stgd->sgjd", probs, value_tiles, preferred_element_type=jnp.float32)
    owner_hits = slot_owner[None, :] == jnp.arange(batch_rows, dtype=jnp.int32)[:, None]
    seq_peak = jnp.max(jnp.where(owner_hits[:, :, None, None], page_peak[None], neg_fill), axis=1)
    factor = jnp.exp(page_peak - jnp.take(seq_peak, slot_owner, axis=0))
    hit_float = owner_hits.astype(jnp.float32)
    heads_local = groups_local * per_group
    seq_mass = jnp.dot(
        hit_float,
        (page_mass * factor).reshape(slot_count, heads_local),
        precision=lax.Precision.HIGHEST,
        preferred_element_type=jnp.float32,
    )
    seq_out = jnp.dot(
        hit_float,
        (page_out * factor[..., None]).reshape(slot_count, heads_local * DH),
        precision=lax.Precision.HIGHEST,
        preferred_element_type=jnp.float32,
    )
    seq_peak = seq_peak.reshape(batch_rows, heads_local)
    top_all = over_copies(seq_peak, ("seq", "sub"))
    rescale = jnp.exp(seq_peak - top_all)
    mass_all = taken_together(seq_mass * rescale, ("seq", "sub"))
    out_part = sum_at_owner(spread(seq_out, rescale), ("seq", "sub"), 1)
    width = out_part.shape[1]
    start = lax.axis_index(("seq", "sub")) * width
    mass_cols = jnp.repeat(mass_all, DH, axis=1)
    mass_part = lax.dynamic_slice_in_dim(mass_cols, start, width, 1)
    attention_part = (out_part / mass_part).astype(jnp.bfloat16)
    attention = gathered_copies(attention_part, ("seq", "sub"), 1)
    partial_out = jnp.dot(attention, out_weight, preferred_element_type=jnp.float32)
    return taken_together(partial_out, "head").astype(jnp.bfloat16)


def solution(mesh):
    in_specs = (
        P("rep", "head"),
        P(("rep", "seq", "sub"), None, "head"),
        P(("rep", "seq", "sub"), None, "head"),
        P("rep"),
        P(("rep", "seq", "sub")),
        P(("rep", "seq", "sub")),
        P("head", ("seq", "sub")),
    )
    out_specs = P("rep", ("seq", "sub"))
    return jax.shard_map(
        on_device, mesh=mesh, in_specs=in_specs, out_specs=out_specs, check_vma=False
    )
```

profile of v0, /device:TPU:65, one launch (start us, length us, event | category | flops | bytes accessed | tf_op | source)
XLA Modules:
  0.0 134.7 jit_solution(5279195749350970024)
XLA Ops:
  0.0 0.0 copy-start
  0.0 0.8 compare_select_fusion
  0.8 0.7 iota_compare_fusion.1
  1.5 1.4 %gather_fusion = s32[64]{0:T(128)S(1)} fusion(s32[16]{0:T(128)} %param.10, s32[1024]{0:T(1024)S(1)} %pad_clamp_fusion), kind=kCustom, calls=%fused_computation | custom fusion | bytes 768 | tf_op jit(solution)/shard_map/jit(_take)/gather | solution.py:68
  2.9 0.7 subtract_clamp_fusion
  3.6 0.1 iota_compare_fusion
  3.7 1.6 %gather_fusion.1 = bf16[64,1024]{1,0:T(8,128)(2,1)S(1)} fusion(bf16[16,1024]{1,0:T(8,128)(2,1)} %param.7, s32[1024]{0:T(1024)S(1)} %pad_clamp_fusion), kind=kCustom, calls=%fused_computation.1 | custom fusion | bytes 262400 | tf_op jit(solution)/shard_map/jit(_take)/gather | solution.py:63
  5.3 0.1 bitcast_select_fusion
  5.4 0.0 copy-done
  5.4 1.3 fusion.7
  6.7 0.1 copy.27
  6.8 0.1 select_reduce_fusion
  6.9 0.1 copy.30
  7.0 0.7 reshape.189
  7.7 45.2 %all-to-all-start = ((f32[32,1,128]{2,1,0:T(1,128)}), f32[32,1,128]{2,1,0:T(1,128)S(1)}, u32[]{:S(2)}, u32[]{:S(2)}) async-start(f32[32,1,128]{2,1,0:T(1,128)} %reshape.189), calls=%async_computation | async-start | bytes 32768 | tf_op jit(solution)/shard_map/all_to_all | solution.py:15
  52.8 0.6 gather_fusion.2
  53.4 0.1 subtract_exponential_fusion
  53.5 2.3 %convolution_multiply_fusion = f32[64,8,128]{2,1,0:T(8,128)S(1)} fusion(bf16[64,128,128]{2,1,0:T(8,128)(2,1)} %param.9, f32[64,8]{1,0:T(8,128)S(1)} %subtract_exponential_fusion, f32[64,8,128]{2,1,0:T(8,128)S(1)} %get-tuple-element.8, f32[64,8]{1,0:T(8,128)S(1)} %get-tuple-element.7), kind=kOutput, calls=%fused_computation.3 | convolution fusion | flops 16973824 | bytes 2625536 | tf_op jit(solution)/shard_map/sgjt,stgd->sgjd/dot_general | solution.py:75
  55.8 0.2 convert_reduce_fusion
  56.1 8.6 %all-to-all-done = f32[32,1,128]{2,1,0:T(1,128)S(1)} async-done(((f32[32,1,128]{2,1,0:T(1,128)}), f32[32,1,128]{2,1,0:T(1,128)S(1)}, u32[]{:S(2)}, u32[]{:S(2)}) %all-to-all-start) | async-done | bytes 16416 | tf_op jit(solution)/shard_map/all_to_all | solution.py:15
  64.7 0.5 broadcast.100
  65.2 0.7 reduce.5
  65.9 0.1 reshape.190
  66.1 0.2 convolution_multiply_fusion.3
  66.3 0.0 copy-start.1
  66.3 0.7 reshape.193
  67.0 4.6 %all-to-all-start.2 = ((f32[32,1,128]{2,1,0:T(1,128)}), f32[32,1,128]{2,1,0:T(1,128)S(1)}, u32[]{:S(2)}, u32[]{:S(2)}) async-start(f32[32,1,128]{2,1,0:T(1,128)} %reshape.193), calls=%async_computation.2 | async-start | bytes 32768 | tf_op jit(solution)/shard_map/all_to_all | solution.py:15
  71.6 0.2 convolution_multiply_fusion.2
  71.9 0.1 reshape_reshape.3
  72.0 0.2 copy.32
  72.1 0.8 reshape.191
  72.9 10.5 %all-to-all-done.2 = f32[32,1,128]{2,1,0:T(1,128)S(1)} async-done(((f32[32,1,128]{2,1,0:T(1,128)}), f32[32,1,128]{2,1,0:T(1,128)S(1)}, u32[]{:S(2)}, u32[]{:S(2)}) %all-to-all-start.2) | async-done | bytes 16416 | tf_op jit(solution)/shard_map/all_to_all | solution.py:15
  83.5 4.6 %all-to-all-start.1 = ((f32[32,1,512]{2,1,0:T(1,128)}), f32[32,1,512]{2,1,0:T(1,128)S(1)}, u32[]{:S(2)}, u32[]{:S(2)}) async-start(f32[32,1,512]{2,1,0:T(1,128)} %reshape.191), calls=%async_computation.1 | async-start | bytes 131072 | tf_op jit(solution)/shard_map/all_to_all | solution.py:38
  88.1 0.7 reduce.7
  88.8 0.1 reshape.194
  88.9 0.1 copy.33
  89.0 0.1 broadcast_in_dim.109
  89.1 12.4 %all-to-all-done.1 = f32[32,1,512]{2,1,0:T(1,128)S(1)} async-done(((f32[32,1,512]{2,1,0:T(1,128)}), f32[32,1,512]{2,1,0:T(1,128)S(1)}, u32[]{:S(2)}, u32[]{:S(2)}) %all-to-all-start.1) | async-done | bytes 65568 | tf_op jit(solution)/shard_map/all_to_all | solution.py:38
  101.5 0.8 reduce.6
  102.3 0.1 reshape.192
  102.5 0.1 divide_convert_fusion
  102.6 0.1 reshape.195
  102.7 16.2 %all_to_all.25 = bf16[32,2,256]{2,1,0:T(2,128)(2,1)S(1)} all-to-all(bf16[32,2,256]{2,1,0:T(2,128)(2,1)S(1)} %reshape.195), channel_id=1, replica_groups=mesh['rep'=2,'seq'=16,'head'=8,'sub'=2] {'seq','sub'}, dimensions={0} | all-to-all | bytes 65536 | tf_op jit(solution)/shard_map/all_to_all | solution.py:15
  118.9 0.1 reshape.196
  119.1 0.2 reshape.156
  119.3 0.2 fusion.8
  119.5 14.6 %all_to_all.26 = f32[8,16,256]{2,1,0:T(8,128)S(1)} all-to-all(f32[8,16,256]{2,1,0:T(8,128)S(1)} %broadcast_in_dim.111), channel_id=1, replica_groups=mesh['rep'=2,'seq'=16,'head'=8,'sub'=2] {'head'}, dimensions={0} | all-to-all | bytes 262144 | tf_op jit(solution)/shard_map/all_to_all | solution.py:15
  134.1 0.6 reduce_sum.39
  (16 shorter events, 0.3 us)
Async XLA Ops:
  0.0 5.4 %copy-start = (bf16[64,128,128]{2,1,0:T(8,128)(2,1)S(1)}, bf16[64,128,128]{2,1,0:T(8,128)(2,1)}, u32[]{:S(2)}) copy-start(bf16[64,128,128]{2,1,0:T(8,128)(2,1)} %param.8) | copy-start | bytes 6291460
  6.7 59.4 %copy-start.2 = (s32[64]{0:T(128)S(1)}, s32[64]{0:T(128)}, u32[]{:S(2)}) copy-start(s32[64]{0:T(128)} %param.11) | copy-start | bytes 772
  7.7 57.0 %all-to-all-start = ((f32[32,1,128]{2,1,0:T(1,128)}), f32[32,1,128]{2,1,0:T(1,128)S(1)}, u32[]{:S(2)}, u32[]{:S(2)}) async-start(f32[32,1,128]{2,1,0:T(1,128)} %reshape.189), calls=%async_computation | async-start | bytes 32768 | tf_op jit(solution)/shard_map/all_to_all | solution.py:15
  66.3 53.0 %copy-start.1 = (bf16[1024,256]{1,0:T(8,128)(2,1)S(1)}, bf16[1024,256]{1,0:T(8,128)(2,1)}, u32[]{:S(2)}) copy-start(bf16[1024,256]{1,0:T(8,128)(2,1)} %param.13) | copy-start | bytes 1572868
  67.0 16.5 %all-to-all-start.2 = ((f32[32,1,128]{2,1,0:T(1,128)}), f32[32,1,128]{2,1,0:T(1,128)S(1)}, u32[]{:S(2)}, u32[]{:S(2)}) async-start(f32[32,1,128]{2,1,0:T(1,128)} %reshape.193), calls=%async_computation.2 | async-start | bytes 32768 | tf_op jit(solution)/shard_map/all_to_all | solution.py:15
  83.5 18.0 %all-to-all-start.1 = ((f32[32,1,512]{2,1,0:T(1,128)}), f32[32,1,512]{2,1,0:T(1,128)S(1)}, u32[]{:S(2)}, u32[]{:S(2)}) async-start(f32[32,1,512]{2,1,0:T(1,128)} %reshape.191), calls=%async_computation.1 | async-start | bytes 131072 | tf_op jit(solution)/shard_map/all_to_all | solution.py:38
where the time goes:
time: 136 us; the launch traced here: 135 us
  starting transfers between devices  54.4 us (40%)
  waiting for transfers between devices  31.6 us (23%)
  blocking collectives  30.8 us (23%)
  local copies, waits for them, and re-layouts  7.77 us (6%)
  other arithmetic  5.78 us (4%)
  matrix products  4.15 us (3%)
    all_to_all x2, starting transfers between devices, copy_for_each(): lax.all_to_all(jnp.broadcast_to(shard[None], (size, *shard.shape)), axis,...  49.8 us
    all_to_all x2, blocking collectives, copy_for_each(): lax.all_to_all(jnp.broadcast_to(shard[None], (size, *shard.shape)), axis,...  30.8 us
    all_to_all x2, waiting for transfers between devices, copy_for_each(): lax.all_to_all(jnp.broadcast_to(shard[None], (size, *shard.shape)), axis,...  19.2 us
    all_to_all x1, waiting for transfers between devices, sum_at_owner(): lax.all_to_all(blocks, axis, split_axis=0, concat_axis=0, tiled=True)  12.4 us
    all_to_all x1, starting transfers between devices, sum_at_owner(): lax.all_to_all(blocks, axis, split_axis=0, concat_axis=0, tiled=True)  4.63 us
    unnamed x18, local copies, waits for them, and re-layouts  2.85 us
  transfers between devices with their start and end apart: 3, of which 3 were waited for; matrix products, arithmetic and copies ran while one was open for 4% of the time, Pallas kernels for 0%

commit v1 on v0

v1 whole, which is shorter than its diff:
```python
import functools

import jax
import jax.numpy as jnp
from jax import lax
from jax.experimental import pallas as pl
from jax.experimental.pallas import tpu as pltpu
from jax.sharding import PartitionSpec as P

DH = 128
PAGE = 128
NEG = -1e30
CHUNKS = 4
F32 = jnp.float32
BF16 = jnp.bfloat16
MESH = pl.DeviceIdType.MESH


def kernel(
    sizes,
    lengths,
    owners,
    numbers,
    owner_row,
    q_ref,
    k_hbm,
    v_hbm,
    w_hbm,
    out_ref,
    k_ref,
    v_ref,
    w_ref,
    q_rows,
    q_seq,
    peaks,
    masses,
    scaled,
    hits,
    seq_lse,
    lse_diag,
    part_out,
    part_lse,
    got_out,
    got_lse,
    half_out,
    half_lse,
    all_out,
    all_lse,
    att_rows,
    proj_mine,
    proj_all,
    k_sem,
    v_sem,
    w_sem,
    a_send,
    a_recv,
    b_send,
    b_recv,
    c_send,
    c_recv,
    far_sem,
):
    n_z, n_x, n_c = sizes
    batch, heads, slots = lengths.shape[0], q_ref.shape[1] // DH, owners.shape[0]
    half = n_z // 2
    near = half // 2
    z, x, c = lax.axis_index("seq"), lax.axis_index("head"), lax.axis_index("sub")
    rows = batch * heads
    per_chunk = slots // CHUNKS

    def ring(offset):
        return lax.rem(z + offset + n_z, n_z)

    def core(j):
        return lax.rem(c + j, n_c)

    loads = []
    for hbm, ref, sem in ((k_hbm, k_ref, k_sem), (v_hbm, v_ref, v_sem)):
        copies = []
        for i in range(CHUNKS):
            span = pl.ds(i * per_chunk, per_chunk)
            copies.append(pltpu.make_async_copy(hbm.at[span], ref.at[span], sem.at[i]))
        loads.append(copies)
    w_load = pltpu.make_async_copy(w_hbm, w_ref, w_sem)
    for copies in loads:
        for copy in copies:
            copy.start()
    w_load.start()

    barrier = pltpu.get_barrier_semaphore()
    greeted = 0
    for dz in range(-near, near + 1):
        for j in range(n_c):
            if dz or j:
                greeted += 1
                pl.semaphore_signal(
                    barrier, inc=1, device_id={"seq": ring(dz), "sub": core(j)}, device_id_type=MESH
                )
    for dx in range(1, n_x):
        greeted += 1
        pl.semaphore_signal(
            barrier, inc=1, device_id={"head": lax.rem(x + dx, n_x)}, device_id_type=MESH
        )

    lane = lax.broadcasted_iota(jnp.int32, (heads, rows), 1)
    sub = lax.broadcasted_iota(jnp.int32, (heads, rows), 0)
    diag = lane - sub

    for h in range(heads):
        q_rows[pl.ds(h, batch, stride=heads), :] = q_ref[:, h * DH : (h + 1) * DH].astype(F32)
    q_seq[...] = q_rows[...].reshape(batch, heads, DH)

    hit = (lax.broadcasted_iota(jnp.int32, (batch, slots), 0) == owner_row[...]).astype(BF16)
    spread_rows = lax.broadcasted_iota(jnp.int32, (slots, slots * heads), 0)
    spread_cols = lax.broadcasted_iota(jnp.int32, (slots, slots * heads), 1)
    spread = (spread_cols // heads == spread_rows).astype(BF16)
    wide = jnp.dot(hit, spread, preferred_element_type=F32)
    wide = jnp.broadcast_to(wide[:, None, :], (batch, heads, slots * heads))
    w_sub = lax.broadcasted_iota(jnp.int32, (batch, heads, slots * heads), 1)
    w_lane = lax.broadcasted_iota(jnp.int32, (batch, heads, slots * heads), 2)
    hits[...] = jnp.where(w_lane % heads == w_sub, wide, 0.0).reshape(rows, slots * heads).astype(BF16)

    scale = 1.0 / (float(DH) ** 0.5)
    pair_sub = lax.broadcasted_iota(jnp.int32, (2 * heads, PAGE), 0)
    pair_lane = lax.broadcasted_iota(jnp.int32, (2 * heads, PAGE), 1)
    first = pair_sub < heads

    probs = []
    top = jnp.full((heads, rows), NEG, F32)
    for i in range(CHUNKS):
        loads[0][i].wait()
        for pair in range(i * per_chunk // 2, (i + 1) * per_chunk // 2):
            a, b = 2 * pair, 2 * pair + 1
            own_a, own_b = owners[a], owners[b]
            q_pair = jnp.concatenate(
                [
                    q_seq[own_a],
                    q_seq[own_b],
                ],
                axis=0,
            ).astype(BF16)
            keys = k_ref[a : b + 1].reshape(2 * PAGE, DH)
            both = lax.dot_general(
                q_pair, keys, (((1,), (1,)), ((), ())), preferred_element_type=F32
            )
            scores = jnp.concatenate([both[:heads, :PAGE], both[heads:, PAGE:]], axis=0) * scale
            live_a = jnp.clip(lengths[own_a] - numbers[a] * PAGE, 0, PAGE)
            live_b = jnp.clip(lengths[own_b] - numbers[b] * PAGE, 0, PAGE)
            scores = jnp.where(pair_lane < jnp.where(first, live_a, live_b), scores, NEG)
            peak = jnp.max(scores, axis=1, keepdims=True)
            prob = jnp.exp(scores - peak).astype(BF16)
            mass = jnp.sum(prob.astype(F32), axis=1, keepdims=True)
            peak = jnp.broadcast_to(peak, (2 * heads, PAGE))
            mass = jnp.broadcast_to(mass, (2 * heads, PAGE))
            peaks[pl.ds(a * heads, 2 * heads), :] = peak
            masses[pl.ds(a * heads, 2 * heads), :] = mass
            probs.append(prob)
            top = jnp.maximum(top, jnp.where(diag == own_a * heads, peak[:heads], NEG))
            top = jnp.maximum(top, jnp.where(diag == own_b * heads, peak[heads:], NEG))

    def by_sequence(row_values):
        for b in range(batch):
            mine = jnp.max(
                jnp.where(lane // heads == b, row_values, 2 * NEG), axis=1, keepdims=True
            )
            seq_lse[b] = jnp.broadcast_to(mine, (heads, rows))

    by_sequence(top)
    total = jnp.zeros((heads, rows), F32)
    for s in range(slots):
        span = pl.ds(s * heads, heads)
        factor = jnp.exp(peaks[span, :] - seq_lse[owners[s]])
        total = total + jnp.where(diag == owners[s] * heads, factor * masses[span, :], 0.0)
    lse = jnp.where(total > 0.0, top + jnp.log(jnp.where(total > 0.0, total, 1.0)), NEG)
    by_sequence(lse)

    for b in range(batch):
        lse_diag[pl.ds(b * heads, heads), :] = jnp.where(lane % heads == sub, seq_lse[b], 0.0)
    tiled = lse_diag[pl.ds(0, batch, stride=heads), :]
    for h in range(1, heads):
        tiled = tiled + lse_diag[pl.ds(h, batch, stride=heads), :]
    part_lse[...] = tiled.reshape(batch, 1, rows)

    for i in range(CHUNKS):
        loads[1][i].wait()
        for pair in range(i * per_chunk // 2, (i + 1) * per_chunk // 2):
            a, b = 2 * pair, 2 * pair + 1
            prob = probs[pair]
            block = jnp.concatenate(
                [
                    jnp.where(first, prob, jnp.zeros_like(prob)),
                    jnp.where(first, jnp.zeros_like(prob), prob),
                ],
                axis=1,
            )
            values = v_ref[a : b + 1].reshape(2 * PAGE, DH)
            page_out = jnp.dot(block, values, preferred_element_type=F32)
            span = pl.ds(a * heads, 2 * heads)
            level = jnp.concatenate([seq_lse[owners[a]], seq_lse[owners[b]]], axis=0)
            factor = jnp.exp(peaks[span, :] - level)
            scaled[span, :] = (page_out * factor).astype(BF16)
    mine = jnp.dot(hits[...], scaled[...], preferred_element_type=F32)
    part_out[...] = mine.astype(BF16).reshape(batch, heads, DH)

    pl.semaphore_wait(barrier, greeted)
    for dz in (-near, near):
        pl.semaphore_signal(far_sem, inc=1, device_id={"seq": ring(dz)}, device_id_type=MESH)

    a_copies = []
    order = sorted(range(-near, near), key=lambda d: -abs(d))
    for dz in order:
        for j in range(n_c):
            target = lax.rem(ring(dz), half) * n_c + core(j)
            slot = (near - 1 - dz) * n_c + j
            if dz == 0 and j == 0:
                got_out[slot] = part_out[target]
                got_lse[pl.ds(slot, 1), :] = part_lse[target]
                continue
            for k, (src, dst) in enumerate(
                ((part_out.at[target], got_out.at[slot]), (part_lse.at[target], got_lse.at[pl.ds(slot, 1), :]))
            ):
                copy = pltpu.make_async_remote_copy(
                    src_ref=src,
                    dst_ref=dst,
                    send_sem=a_send.at[slot, k],
                    recv_sem=a_recv.at[slot, k],
                    device_id={"seq": ring(dz), "sub": core(j)},
                    device_id_type=MESH,
                )
                copy.start()
                a_copies.append(copy)
    for copy in a_copies:
        copy.wait_recv()

    sources = half * n_c
    levels = got_lse[...]
    peak = jnp.max(levels, axis=0, keepdims=True)
    weight = jnp.exp(levels - peak)
    norm = jnp.sum(weight, axis=0, keepdims=True)
    weight = weight / norm
    s_sub = lax.broadcasted_iota(jnp.int32, (sources, sources * heads), 0)
    s_lane = lax.broadcasted_iota(jnp.int32, (sources, sources * heads), 1)
    flat = jnp.sum(jnp.where(s_lane // heads == s_sub, weight, 0.0), axis=0, keepdims=True)
    mix = jnp.where(lane % heads == sub, jnp.broadcast_to(flat, (heads, rows)), 0.0)
    high = mix.astype(BF16)
    low = (mix - high.astype(F32)).astype(BF16)
    both = jnp.dot(
        jnp.concatenate([high, low], axis=0),
        got_out[...].reshape(sources * heads, DH),
        preferred_element_type=F32,
    )
    half_out[...] = (both[:heads] + both[heads:]).astype(BF16)
    half_lse[...] = peak + jnp.log(norm)

    pl.semaphore_wait(far_sem, 2)
    b_slot = lax.div(z, half) * batch + lax.rem(z, half) * n_c + c
    all_out[b_slot] = half_out[...]
    all_lse[pl.ds(b_slot, 1), :] = half_lse[...]
    b_copies = []
    order = sorted(range(-half + 1, half + 1), key=lambda d: -abs(d))
    for dz in order:
        for j in range(n_c):
            if dz == 0 and j == 0:
                continue
            index = (dz + half - 1) * n_c + j
            for k, (src, dst) in enumerate(
                ((half_out, all_out.at[b_slot]), (half_lse, all_lse.at[pl.ds(b_slot, 1), :]))
            ):
                copy = pltpu.make_async_remote_copy(
                    src_ref=src,
                    dst_ref=dst,
                    send_sem=b_send.at[index, k],
                    recv_sem=b_recv.at[index, k],
                    device_id={"seq": ring(dz), "sub": core(j)},
                    device_id_type=MESH,
                )
                copy.start()
                b_copies.append(copy)
    w_load.wait()
    for copy in b_copies:
        copy.wait_recv()

    l_one, l_two = all_lse[:batch, :], all_lse[batch:, :]
    peak = jnp.maximum(l_one, l_two)
    w_one, w_two = jnp.exp(l_one - peak), jnp.exp(l_two - peak)
    inv = 1.0 / (w_one + w_two)
    spot = lax.broadcasted_iota(jnp.int32, (batch, heads, rows), 0) * heads
    spot = spot + lax.broadcasted_iota(jnp.int32, (batch, heads, rows), 1)
    here = lax.broadcasted_iota(jnp.int32, (batch, heads, rows), 2) == spot
    blocks = []
    for weight in (w_one * inv, w_two * inv):
        expanded = jnp.broadcast_to(weight[:, None, :], (batch, heads, rows))
        blocks.append(jnp.where(here, expanded, 0.0).reshape(rows, rows))
    mix = jnp.concatenate(blocks, axis=1)
    high = mix.astype(BF16)
    low = (mix - high.astype(F32)).astype(BF16)
    parts = all_out[...].reshape(2 * rows, DH)
    att_rows[...] = jnp.dot(high, parts, preferred_element_type=F32) + jnp.dot(
        low, parts, preferred_element_type=F32
    )
    attention = jnp.concatenate(
        [att_rows[pl.ds(h, batch, stride=heads), :] for h in range(heads)], axis=1
    ).astype(BF16)
    projected = jnp.dot(attention, w_ref[...], preferred_element_type=F32)
    proj_mine[...] = projected.astype(BF16)
    proj_all[x] = proj_mine[...]

    c_copies = []
    for dx in sorted(range(1, n_x), key=lambda d: -min(d, n_x - d)):
        copy = pltpu.make_async_remote_copy(
            src_ref=proj_mine,
            dst_ref=proj_all.at[x],
            send_sem=c_send.at[dx - 1],
            recv_sem=c_recv.at[dx - 1],
            device_id={"head": lax.rem(x + dx, n_x)},
            device_id_type=MESH,
        )
        copy.start()
        c_copies.append(copy)
    for copy in c_copies:
        copy.wait_recv()
    summed = proj_all[0].astype(F32)
    for i in range(1, n_x):
        summed = summed + proj_all[i].astype(F32)
    out_ref[...] = summed.astype(out_ref.dtype)
    for copy in a_copies + b_copies + c_copies:
        copy.wait_send()


def on_device(sizes, queries, key_cache, value_cache, seq_lengths, slot_owner, slot_page, out_weight):
    n_z, n_x, n_c = sizes
    batch, heads = queries.shape[0], queries.shape[1] // DH
    slots = key_cache.shape[0]
    rows = batch * heads
    width = out_weight.shape[1]
    sources = n_z // 2 * n_c
    assert key_cache.shape[2] == DH and sources == batch and rows == DH
    vmem = pl.BlockSpec(memory_space=pltpu.VMEM)
    smem = pl.BlockSpec(memory_space=pltpu.SMEM)
    hbm = pl.BlockSpec(memory_space=pltpu.HBM)
    dma = pltpu.SemaphoreType.DMA
    return pl.pallas_call(
        functools.partial(kernel, sizes),
        out_shape=jax.ShapeDtypeStruct((batch, width), BF16),
        in_specs=[smem, smem, smem, vmem, vmem, hbm, hbm, hbm],
        out_specs=vmem,
        scratch_shapes=[
            pltpu.VMEM(key_cache.shape, BF16),
            pltpu.VMEM(value_cache.shape, BF16),
            pltpu.VMEM(out_weight.shape, BF16),
            pltpu.VMEM((rows, DH), F32),
            pltpu.VMEM((batch, heads, DH), F32),
            pltpu.VMEM((slots * heads, PAGE), F32),
            pltpu.VMEM((slots * heads, PAGE), F32),
            pltpu.VMEM((slots * heads, DH), BF16),
            pltpu.VMEM((rows, slots * heads), BF16),
            pltpu.VMEM((batch, heads, rows), F32),
            pltpu.VMEM((rows, rows), F32),
            pltpu.VMEM((batch, heads, DH), BF16),
            pltpu.VMEM((batch, 1, rows), F32),
            pltpu.VMEM((sources, heads, DH), BF16),
            pltpu.VMEM((sources, rows), F32),
            pltpu.VMEM((heads, DH), BF16),
            pltpu.VMEM((1, rows), F32),
            pltpu.VMEM((2 * batch, heads, DH), BF16),
            pltpu.VMEM((2 * batch, rows), F32),
            pltpu.VMEM((rows, DH), F32),
            pltpu.VMEM((batch, width), BF16),
            pltpu.VMEM((n_x, batch, width), BF16),
            dma((CHUNKS,)),
            dma((CHUNKS,)),
            dma,
            dma((sources, 2)),
            dma((sources, 2)),
            dma((n_z * n_c, 2)),
            dma((n_z * n_c, 2)),
            dma((n_x - 1,)),
            dma((n_x - 1,)),
            pltpu.SemaphoreType.REGULAR,
        ],
        compiler_params=pltpu.CompilerParams(collective_id=0, has_side_effects=True),
        name="decode",
    )(
        seq_lengths,
        slot_owner,
        slot_page,
        slot_owner.reshape(1, slots),
        queries,
        key_cache,
        value_cache,
        out_weight,
    )


def solution(mesh):
    sizes = (mesh.shape["seq"], mesh.shape["head"], mesh.shape["sub"])
    in_specs = (
        P("rep", "head"),
        P(("rep", "seq", "sub"), None, "head"),
        P(("rep", "seq", "sub"), None, "head"),
        P("rep"),
        P(("rep", "seq", "sub")),
        P(("rep", "seq", "sub")),
        P("head", ("seq", "sub")),
    )
    out_specs = P("rep", ("seq", "sub"))
    return jax.shard_map(
        functools.partial(on_device, sizes),
        mesh=mesh,
        in_specs=in_specs,
        out_specs=out_specs,
        check_vma=False,
    )
```

time: 136 us -> 69.6 us (0.51)
  Pallas kernels: 0 us -> 68 us
  starting transfers between devices: 54.4 us -> 0 us
  waiting for transfers between devices: 31.6 us -> 0 us
  blocking collectives: 30.8 us -> 0 us
  local copies, waits for them, and re-layouts: 7.77 us -> 1.3 us
  other arithmetic: 5.78 us -> 0 us
  matrix products: 4.15 us -> 0 us
    pallas_call x0 -> x1, Pallas kernels: none -> 68 us  [on_device(): pl.pallas_call(functools.partial(kernel, sizes), out_shape=jax.ShapeDtype...]
    all_to_all x3 -> x0, starting transfers between devices: 54.4 us -> none  [the longest x2 49.8 us: copy_for_each(): lax.all_to_all(jnp.broadcast_to(shard[None], (size, *shard.shape)), axis,...]
    all_to_all x3 -> x0, waiting for transfers between devices: 31.6 us -> none  [the longest x2 19.2 us: copy_for_each(): lax.all_to_all(jnp.broadcast_to(shard[None], (size, *shard.shape)), axis,...]
    all_to_all x2 -> x0, blocking collectives: 30.8 us -> none  [copy_for_each(): lax.all_to_all(jnp.broadcast_to(shard[None], (size, *shard.shape)), axis,...]
    dot_general x5 -> x0, matrix products: 4.15 us -> none  [the longest x1 2.3 us: on_device(): jnp.einsum('sgjt,stgd->sgjd', probs, value_tiles, preferred_element_type=...]
    gather x3 -> x0, local copies, waits for them, and re-layouts: 3.59 us -> none  [the longest x1 1.56 us: on_device(): jnp.take(queries, slot_owner, axis=0)]
    all_to_all x3 -> x0, other arithmetic: 2.17 us -> none  [the longest x2 1.37 us: copy_for_each(): lax.all_to_all(jnp.broadcast_to(shard[None], (size, *shard.shape)), axis,...]
    unnamed x18 -> x1, local copies, waits for them, and re-layouts: 2.85 us -> 1.3 us
  transfers between devices with their start and end apart: 3 -> 0, of which waited for: 3 -> 0; matrix products, arithmetic and copies ran while one was open for 4% -> 0% of each run, Pallas kernels for 0% -> 0%
where the time goes in v1:
time: 69.6 us; the launch traced here: 69.3 us
  Pallas kernels  68 us (98%)
  local copies, waits for them, and re-layouts  1.3 us (2%)
    pallas_call x1, Pallas kernels, on_device(): pl.pallas_call(functools.partial(kernel, sizes), out_shape=jax.ShapeDtype...  68 us

profile of v1, /device:TPU:65, one launch (start us, length us, event | category | flops | bytes accessed | tf_op | source)
XLA Modules:
  0.0 69.3 jit_solution(1882051817096470219)
XLA Ops:
  0.0 68.0 %decode.1 = bf16[16,256]{1,0:T(8,128)(2,1)} custom-call(s32[16]{0:T(128)} %lengths.1, s32[64]{0:T(128)} %owners.1, s32[64]{0:T(128)} %numbers.1, s32[1,64]{1,0:T(1,128)} %bitcast.1, bf16[16,1024]{1,0:T(8,128)(2,1)} %q_ref.1, bf16[64,128,128]{2,1,0:T(8,128)(2,1)} %k_hbm.1, bf16[64,128,128]{2,1,0:T(8,128)(2,1)} %v_hbm.1, bf16[1024,256]{1,0:T(8,128)(2,1)} %w_hbm.1), custom_call_target="tpu_custom_call" | custom-call | tf_op jit(solution)/shard_map/decode/pallas_call | solution.py:342
  68.0 1.3 %copy.9 = bf16[16,256]{1,0:T(8,128)(2,1)} copy(bf16[16,256]{1,0:T(8,128)(2,1)} %decode.1) | data formatting | bytes 16384

commit v2 on v1

--- a/solution.py
+++ b/solution.py
@@ -18,15 +18,20 @@
 
 def kernel(
     sizes,
+    lengths_hbm,
+    owners_hbm,
+    numbers_hbm,
+    owner_row_hbm,
+    q_hbm,
+    k_hbm,
+    v_hbm,
+    w_hbm,
+    out_ref,
     lengths,
     owners,
     numbers,
     owner_row,
     q_ref,
-    k_hbm,
-    v_hbm,
-    w_hbm,
-    out_ref,
     k_ref,
     v_ref,
     w_ref,
@@ -34,7 +39,6 @@
     q_seq,
     peaks,
     masses,
-    scaled,
     hits,
     seq_lse,
     lse_diag,
@@ -49,6 +53,7 @@
     att_rows,
     proj_mine,
     proj_all,
+    small_sem,
     k_sem,
     v_sem,
     w_sem,
@@ -74,6 +79,18 @@
     def core(j):
         return lax.rem(c + j, n_c)
 
+    small = [
+        pltpu.make_async_copy(src, dst, small_sem.at[i])
+        for i, (src, dst) in enumerate(
+            (
+                (owners_hbm, owners),
+                (lengths_hbm, lengths),
+                (numbers_hbm, numbers),
+                (owner_row_hbm, owner_row),
+                (q_hbm, q_ref),
+            )
+        )
+    ]
     loads = []
     for hbm, ref, sem in ((k_hbm, k_ref, k_sem), (v_hbm, v_ref, v_sem)):
         copies = []
@@ -82,14 +99,16 @@
             copies.append(pltpu.make_async_copy(hbm.at[span], ref.at[span], sem.at[i]))
         loads.append(copies)
     w_load = pltpu.make_async_copy(w_hbm, w_ref, w_sem)
-    for copies in loads:
-        for copy in copies:
-            copy.start()
-    w_load.start()
+    for copy in small + loads[0]:
+        copy.start()
+
+    def wait_all(ref, count, sem):
+        span = ref.at[pl.ds(0, count)]
+        pltpu.make_async_copy(span, span, sem).wait()
 
     barrier = pltpu.get_barrier_semaphore()
     greeted = 0
-    for dz in range(-near, near + 1):
+    for dz in sorted(range(-near, near + 1), key=lambda d: -abs(d)):
         for j in range(n_c):
             if dz or j:
                 greeted += 1
@@ -101,6 +120,11 @@
         pl.semaphore_signal(
             barrier, inc=1, device_id={"head": lax.rem(x + dx, n_x)}, device_id_type=MESH
         )
+
+    for copy in loads[1] + [w_load]:
+        copy.start()
+    for copy in small:
+        copy.wait()
 
     lane = lax.broadcasted_iota(jnp.int32, (heads, rows), 1)
     sub = lax.broadcasted_iota(jnp.int32, (heads, rows), 0)
@@ -181,8 +205,10 @@
         tiled = tiled + lse_diag[pl.ds(h, batch, stride=heads), :]
     part_lse[...] = tiled.reshape(batch, 1, rows)
 
+    mine = jnp.zeros((rows, DH), F32)
     for i in range(CHUNKS):
         loads[1][i].wait()
+        high, low = [], []
         for pair in range(i * per_chunk // 2, (i + 1) * per_chunk // 2):
             a, b = 2 * pair, 2 * pair + 1
             prob = probs[pair]
@@ -198,15 +224,19 @@
             span = pl.ds(a * heads, 2 * heads)
             level = jnp.concatenate([seq_lse[owners[a]], seq_lse[owners[b]]], axis=0)
             factor = jnp.exp(peaks[span, :] - level)
-            scaled[span, :] = (page_out * factor).astype(BF16)
-    mine = jnp.dot(hits[...], scaled[...], preferred_element_type=F32)
+            page_out = page_out * factor
+            high.append(page_out.astype(BF16))
+            low.append((page_out - high[-1].astype(F32)).astype(BF16))
+        hit = hits[:, i * per_chunk * heads : (i + 1) * per_chunk * heads]
+        mine = mine + jnp.dot(
+            jnp.concatenate([hit, hit], axis=1),
+            jnp.concatenate(high + low, axis=0),
+            preferred_element_type=F32,
+        )
     part_out[...] = mine.astype(BF16).reshape(batch, heads, DH)
 
     pl.semaphore_wait(barrier, greeted)
-    for dz in (-near, near):
-        pl.semaphore_signal(far_sem, inc=1, device_id={"seq": ring(dz)}, device_id_type=MESH)
-
-    a_copies = []
+    a_count = 0
     order = sorted(range(-near, near), key=lambda d: -abs(d))
     for dz in order:
         for j in range(n_c):
@@ -222,15 +252,17 @@
                 copy = pltpu.make_async_remote_copy(
                     src_ref=src,
                     dst_ref=dst,
-                    send_sem=a_send.at[slot, k],
-                    recv_sem=a_recv.at[slot, k],
+                    send_sem=a_send.at[k],
+                    recv_sem=a_recv.at[k],
                     device_id={"seq": ring(dz), "sub": core(j)},
                     device_id_type=MESH,
                 )
                 copy.start()
-                a_copies.append(copy)
-    for copy in a_copies:
-        copy.wait_recv()
+            a_count += 1
+    for dz in (-near, near):
+        pl.semaphore_signal(far_sem, inc=1, device_id={"seq": ring(dz)}, device_id_type=MESH)
+    wait_all(got_lse, a_count, a_recv.at[1])
+    wait_all(got_out, a_count, a_recv.at[0])
 
     sources = half * n_c
     levels = got_lse[...]
@@ -256,29 +288,30 @@
     b_slot = lax.div(z, half) * batch + lax.rem(z, half) * n_c + c
     all_out[b_slot] = half_out[...]
     all_lse[pl.ds(b_slot, 1), :] = half_lse[...]
-    b_copies = []
+    b_count = 0
     order = sorted(range(-half + 1, half + 1), key=lambda d: -abs(d))
     for dz in order:
         for j in range(n_c):
             if dz == 0 and j == 0:
                 continue
-            index = (dz + half - 1) * n_c + j
             for k, (src, dst) in enumerate(
                 ((half_out, all_out.at[b_slot]), (half_lse, all_lse.at[pl.ds(b_slot, 1), :]))
             ):
                 copy = pltpu.make_async_remote_copy(
                     src_ref=src,
                     dst_ref=dst,
-                    send_sem=b_send.at[index, k],
-                    recv_sem=b_recv.at[index, k],
+                    send_sem=b_send.at[k],
+                    recv_sem=b_recv.at[k],
                     device_id={"seq": ring(dz), "sub": core(j)},
                     device_id_type=MESH,
                 )
                 copy.start()
-                b_copies.append(copy)
+            b_count += 1
     w_load.wait()
-    for copy in b_copies:
-        copy.wait_recv()
+    wait_all(part_lse, a_count, a_send.at[1])
+    wait_all(part_out, a_count, a_send.at[0])
+    wait_all(all_lse, b_count, b_recv.at[1])
+    wait_all(all_out, b_count, b_recv.at[0])
 
     l_one, l_two = all_lse[:batch, :], all_lse[batch:, :]
     peak = jnp.maximum(l_one, l_two)
@@ -305,26 +338,24 @@
     proj_mine[...] = projected.astype(BF16)
     proj_all[x] = proj_mine[...]
 
-    c_copies = []
     for dx in sorted(range(1, n_x), key=lambda d: -min(d, n_x - d)):
         copy = pltpu.make_async_remote_copy(
             src_ref=proj_mine,
             dst_ref=proj_all.at[x],
-            send_sem=c_send.at[dx - 1],
-            recv_sem=c_recv.at[dx - 1],
+            send_sem=c_send,
+            recv_sem=c_recv,
             device_id={"head": lax.rem(x + dx, n_x)},
             device_id_type=MESH,
         )
         copy.start()
-        c_copies.append(copy)
-    for copy in c_copies:
-        copy.wait_recv()
+    wait_all(all_lse, b_count, b_send.at[1])
+    wait_all(all_out, b_count, b_send.at[0])
+    wait_all(proj_all, n_x - 1, c_send)
+    wait_all(proj_all, n_x - 1, c_recv)
     summed = proj_all[0].astype(F32)
     for i in range(1, n_x):
         summed = summed + proj_all[i].astype(F32)
     out_ref[...] = summed.astype(out_ref.dtype)
-    for copy in a_copies + b_copies + c_copies:
-        copy.wait_send()
 
 
 def on_device(sizes, queries, key_cache, value_cache, seq_lengths, slot_owner, slot_page, out_weight):
@@ -335,16 +366,19 @@
     width = out_weight.shape[1]
     sources = n_z // 2 * n_c
     assert key_cache.shape[2] == DH and sources == batch and rows == DH
-    vmem = pl.BlockSpec(memory_space=pltpu.VMEM)
-    smem = pl.BlockSpec(memory_space=pltpu.SMEM)
     hbm = pl.BlockSpec(memory_space=pltpu.HBM)
     dma = pltpu.SemaphoreType.DMA
     return pl.pallas_call(
         functools.partial(kernel, sizes),
-        out_shape=jax.ShapeDtypeStruct((batch, width), BF16),
-        in_specs=[smem, smem, smem, vmem, vmem, hbm, hbm, hbm],
-        out_specs=vmem,
+        out_shape=pltpu.VMEM((batch, width), BF16),
+        in_specs=[hbm] * 8,
+        out_specs=pl.BlockSpec(memory_space=pltpu.VMEM),
         scratch_shapes=[
+            pltpu.SMEM((batch,), jnp.int32),
+            pltpu.SMEM((slots,), jnp.int32),
+            pltpu.SMEM((slots,), jnp.int32),
+            pltpu.VMEM((1, slots), jnp.int32),
+            pltpu.VMEM(queries.shape, BF16),
             pltpu.VMEM(key_cache.shape, BF16),
             pltpu.VMEM(value_cache.shape, BF16),
             pltpu.VMEM(out_weight.shape, BF16),
@@ -352,7 +386,6 @@
             pltpu.VMEM((batch, heads, DH), F32),
             pltpu.VMEM((slots * heads, PAGE), F32),
             pltpu.VMEM((slots * heads, PAGE), F32),
-            pltpu.VMEM((slots * heads, DH), BF16),
             pltpu.VMEM((rows, slots * heads), BF16),
             pltpu.VMEM((batch, heads, rows), F32),
             pltpu.VMEM((rows, rows), F32),
@@ -367,15 +400,16 @@
             pltpu.VMEM((rows, DH), F32),
             pltpu.VMEM((batch, width), BF16),
             pltpu.VMEM((n_x, batch, width), BF16),
+            dma((5,)),
             dma((CHUNKS,)),
             dma((CHUNKS,)),
             dma,
-            dma((sources, 2)),
-            dma((sources, 2)),
-            dma((n_z * n_c, 2)),
-            dma((n_z * n_c, 2)),
-            dma((n_x - 1,)),
-            dma((n_x - 1,)),
+            dma((2,)),
+            dma((2,)),
+            dma((2,)),
+            dma((2,)),
+            dma,
+            dma,
             pltpu.SemaphoreType.REGULAR,
         ],
         compiler_params=pltpu.CompilerParams(collective_id=0, has_side_effects=True),

time: 69.6 us -> 66.1 us (0.950)
  Pallas kernels: 68 us -> 65.4 us
  local copies, waits for them, and re-layouts: 1.3 us -> 0.6 us
    pallas_call x1, Pallas kernels: 68 us -> 65.4 us  [on_device(): pl.pallas_call(functools.partial(kernel, sizes), out_shape=pltpu.VMEM((ba...]
where the time goes in v2:
time: 66.1 us; the launch traced here: 66 us
  Pallas kernels  65.4 us (99%)
    pallas_call x1, Pallas kernels, on_device(): pl.pallas_call(functools.partial(kernel, sizes), out_shape=pltpu.VMEM((ba...  65.4 us

profile of v2, /device:TPU:65, one launch (start us, length us, event | category | flops | bytes accessed | tf_op | source)
XLA Modules:
  0.0 66.0 jit_solution(15296895150946162572)
XLA Ops:
  0.0 65.4 %decode.1 = bf16[16,256]{1,0:T(8,128)(2,1)S(1)} custom-call(s32[16]{0:T(128)} %lengths_hbm.1, s32[64]{0:T(128)} %owners_hbm.1, s32[64]{0:T(128)} %numbers_hbm.1, s32[1,64]{1,0:T(1,128)} %bitcast.1, bf16[16,1024]{1,0:T(8,128)(2,1)} %q_hbm.1, bf16[64,128,128]{2,1,0:T(8,128)(2,1)} %k_hbm.1, bf16[64,128,128]{2,1,0:T(8,128)(2,1)} %v_hbm.1, bf16[1024,256]{1,0:T(8,128)(2,1)} %w_hbm.1), custom_call_target="tpu_custom_call" | custom-call | tf_op jit(solution)/shard_map/decode/pallas_call | solution.py:371
  65.4 0.6 copy.9

commit v3 on v2

v3 whole, which is shorter than its diff:
```python
import functools

import jax
import jax.numpy as jnp
from jax import lax
from jax.experimental import pallas as pl
from jax.experimental.pallas import tpu as pltpu
from jax.sharding import PartitionSpec as P

DH = 128
PAGE = 128
NEG = -1e30
COPIES = 2
F32 = jnp.float32
BF16 = jnp.bfloat16
MESH = pl.DeviceIdType.MESH


def kernel(
    sizes,
    lengths_hbm,
    owners_hbm,
    numbers_hbm,
    owner_row_hbm,
    q_hbm,
    k_hbm,
    v_hbm,
    w_hbm,
    out_ref,
    lengths,
    owners,
    numbers,
    owner_row,
    q_ref,
    k_ref,
    v_ref,
    w_ref,
    q_rows,
    q_seq,
    peaks,
    masses,
    hits,
    seq_lse,
    lse_diag,
    part_out,
    part_lse,
    got_out,
    got_lse,
    own_out,
    own_lse,
    all_out,
    all_lse,
    att_rows,
    proj_mine,
    proj_all,
    small_sem,
    k_sem,
    v_sem,
    w_sem,
    a_send,
    a_recv,
    b_send,
    b_recv,
    c_send,
    c_recv,
    far_sem,
    side_sem,
):
    n_z, n_x, n_c = sizes
    batch, heads, slots = lengths.shape[0], q_ref.shape[1] // DH, owners.shape[0]
    half = n_z // 2
    near = half // 2
    seg = n_z // COPIES
    per = batch // (seg * n_c)
    sources = seg * n_c
    z, x, c = lax.axis_index("seq"), lax.axis_index("head"), lax.axis_index("sub")
    rows = batch * heads

    def ring(offset):
        return lax.rem(z + offset + n_z, n_z)

    def core(j):
        return lax.rem(c + j, n_c)

    small = [
        pltpu.make_async_copy(src, dst, small_sem.at[i])
        for i, (src, dst) in enumerate(
            (
                (owners_hbm, owners),
                (lengths_hbm, lengths),
                (numbers_hbm, numbers),
                (owner_row_hbm, owner_row),
                (q_hbm, q_ref),
            )
        )
    ]
    k_load = pltpu.make_async_copy(k_hbm, k_ref, k_sem)
    v_load = pltpu.make_async_copy(v_hbm, v_ref, v_sem)
    w_load = pltpu.make_async_copy(w_hbm, w_ref, w_sem)
    for copy in small + [k_load, v_load, w_load]:
        copy.start()

    def wait_all(ref, count, sem):
        span = ref.at[pl.ds(0, count)]
        pltpu.make_async_copy(span, span, sem).wait()

    barrier = pltpu.get_barrier_semaphore()
    greeted = 0
    for dz in sorted(range(-near, near + 1), key=lambda d: -abs(d)):
        for j in range(n_c):
            if dz or j:
                greeted += 1
                pl.semaphore_signal(
                    barrier, inc=1, device_id={"seq": ring(dz), "sub": core(j)}, device_id_type=MESH
                )
    for dx in (1, n_x - 1):
        greeted += 1
        pl.semaphore_signal(
            barrier, inc=1, device_id={"head": lax.rem(x + dx, n_x)}, device_id_type=MESH
        )

    for copy in small:
        copy.wait()

    lane = lax.broadcasted_iota(jnp.int32, (heads, rows), 1)
    sub = lax.broadcasted_iota(jnp.int32, (heads, rows), 0)
    diag = lane - sub

    for h in range(heads):
        q_rows[pl.ds(h, batch, stride=heads), :] = q_ref[:, h * DH : (h + 1) * DH].astype(F32)
    q_seq[...] = q_rows[...].reshape(batch, heads, DH)

    hit = (lax.broadcasted_iota(jnp.int32, (batch, slots), 0) == owner_row[...]).astype(BF16)
    spread_rows = lax.broadcasted_iota(jnp.int32, (slots, slots * heads), 0)
    spread_cols = lax.broadcasted_iota(jnp.int32, (slots, slots * heads), 1)
    spread = (spread_cols // heads == spread_rows).astype(BF16)
    wide = jnp.dot(hit, spread, preferred_element_type=F32)
    wide = jnp.broadcast_to(wide[:, None, :], (batch, heads, slots * heads))
    w_sub = lax.broadcasted_iota(jnp.int32, (batch, heads, slots * heads), 1)
    w_lane = lax.broadcasted_iota(jnp.int32, (batch, heads, slots * heads), 2)
    hits[...] = jnp.where(w_lane % heads == w_sub, wide, 0.0).reshape(rows, slots * heads).astype(BF16)

    scale = 1.0 / (float(DH) ** 0.5)
    pair_sub = lax.broadcasted_iota(jnp.int32, (2 * heads, PAGE), 0)
    pair_lane = lax.broadcasted_iota(jnp.int32, (2 * heads, PAGE), 1)
    first = pair_sub < heads

    probs = []
    top = jnp.full((heads, rows), NEG, F32)
    k_load.wait()
    for pair in range(slots // 2):
        a, b = 2 * pair, 2 * pair + 1
        own_a, own_b = owners[a], owners[b]
        q_pair = jnp.concatenate(
            [
                q_seq[own_a],
                q_seq[own_b],
            ],
            axis=0,
        ).astype(BF16)
        keys = k_ref[a : b + 1].reshape(2 * PAGE, DH)
        both = lax.dot_general(
            q_pair, keys, (((1,), (1,)), ((), ())), preferred_element_type=F32
        )
        scores = jnp.concatenate([both[:heads, :PAGE], both[heads:, PAGE:]], axis=0) * scale
        live_a = jnp.clip(lengths[own_a] - numbers[a] * PAGE, 0, PAGE)
        live_b = jnp.clip(lengths[own_b] - numbers[b] * PAGE, 0, PAGE)
        scores = jnp.where(pair_lane < jnp.where(first, live_a, live_b), scores, NEG)
        peak = jnp.max(scores, axis=1, keepdims=True)
        prob = jnp.exp(scores - peak).astype(BF16)
        mass = jnp.sum(prob.astype(F32), axis=1, keepdims=True)
        peak = jnp.broadcast_to(peak, (2 * heads, PAGE))
        mass = jnp.broadcast_to(mass, (2 * heads, PAGE))
        peaks[pl.ds(a * heads, 2 * heads), :] = peak
        masses[pl.ds(a * heads, 2 * heads), :] = mass
        probs.append(prob)
        top = jnp.maximum(top, jnp.where(diag == own_a * heads, peak[:heads], NEG))
        top = jnp.maximum(top, jnp.where(diag == own_b * heads, peak[heads:], NEG))

    v_load.wait()

    def by_sequence(row_values):
        for b in range(batch):
            mine = jnp.max(
                jnp.where(lane // heads == b, row_values, 2 * NEG), axis=1, keepdims=True
            )
            seq_lse[b] = jnp.broadcast_to(mine, (heads, rows))

    by_sequence(top)
    total = jnp.zeros((heads, rows), F32)
    for s in range(slots):
        span = pl.ds(s * heads, heads)
        factor = jnp.exp(peaks[span, :] - seq_lse[owners[s]])
        total = total + jnp.where(diag == owners[s] * heads, factor * masses[span, :], 0.0)
    lse = jnp.where(total > 0.0, top + jnp.log(jnp.where(total > 0.0, total, 1.0)), NEG)
    by_sequence(lse)

    for b in range(batch):
        lse_diag[pl.ds(b * heads, heads), :] = jnp.where(lane % heads == sub, seq_lse[b], 0.0)
    tiled = lse_diag[pl.ds(0, batch, stride=heads), :]
    for h in range(1, heads):
        tiled = tiled + lse_diag[pl.ds(h, batch, stride=heads), :]
    part_lse[...] = tiled

    high, low = [], []
    for pair in range(slots // 2):
        a, b = 2 * pair, 2 * pair + 1
        prob = probs[pair]
        block = jnp.concatenate(
            [
                jnp.where(first, prob, jnp.zeros_like(prob)),
                jnp.where(first, jnp.zeros_like(prob), prob),
            ],
            axis=1,
        )
        values = v_ref[a : b + 1].reshape(2 * PAGE, DH)
        page_out = jnp.dot(block, values, preferred_element_type=F32)
        span = pl.ds(a * heads, 2 * heads)
        level = jnp.concatenate([seq_lse[owners[a]], seq_lse[owners[b]]], axis=0)
        factor = jnp.exp(peaks[span, :] - level)
        page_out = page_out * factor
        high.append(page_out.astype(BF16))
        low.append((page_out - high[-1].astype(F32)).astype(BF16))
    hit = hits[...]
    mine = jnp.dot(hit, jnp.concatenate(high, axis=0), preferred_element_type=F32)
    mine = mine + jnp.dot(hit, jnp.concatenate(low, axis=0), preferred_element_type=F32)
    part_out[...] = mine.astype(BF16).reshape(batch // per, per, heads, DH)

    pl.semaphore_wait(barrier, greeted)
    a_count = 0
    for dz in sorted(range(-(seg // 2), seg // 2), key=lambda d: -abs(d)):
        for j in range(n_c):
            target = lax.rem(ring(dz), seg) * n_c + core(j)
            slot = (seg // 2 - 1 - dz) * n_c + j
            src_rows, dst_rows = pl.ds(target * per, per), pl.ds(slot * per, per)
            if dz == 0 and j == 0:
                got_out[slot] = part_out[target]
                got_lse[dst_rows, :] = part_lse[src_rows, :]
                continue
            for k, (src, dst) in enumerate(
                (
                    (part_out.at[target], got_out.at[slot]),
                    (part_lse.at[src_rows, :], got_lse.at[dst_rows, :]),
                )
            ):
                copy = pltpu.make_async_remote_copy(
                    src_ref=src,
                    dst_ref=dst,
                    send_sem=a_send.at[k],
                    recv_sem=a_recv.at[k],
                    device_id={"seq": ring(dz), "sub": core(j)},
                    device_id_type=MESH,
                )
                copy.start()
            a_count += 1
    for dz in (-near, near):
        pl.semaphore_signal(far_sem, inc=1, device_id={"seq": ring(dz)}, device_id_type=MESH)
    for dx in (1, n_x - 1):
        pl.semaphore_signal(
            side_sem.at[0], inc=1, device_id={"head": lax.rem(x + dx, n_x)}, device_id_type=MESH
        )
    wait_all(got_lse, a_count * per, a_recv.at[1])
    wait_all(got_out, a_count, a_recv.at[0])

    s_sub = lax.broadcasted_iota(jnp.int32, (sources, rows), 0)
    s_lane = lax.broadcasted_iota(jnp.int32, (sources, rows), 1)
    mixes = []
    for i in range(per):
        levels = got_lse[pl.ds(i, sources, stride=per), :]
        peak = jnp.max(levels, axis=0, keepdims=True)
        weight = jnp.exp(levels - peak)
        norm = jnp.sum(weight, axis=0, keepdims=True)
        weight = weight / norm
        flat = jnp.sum(
            jnp.where(s_lane // heads == s_sub * per + i, weight, 0.0), axis=0, keepdims=True
        )
        mixes.append(jnp.where(lane % heads == sub, jnp.broadcast_to(flat, (heads, rows)), 0.0))
        own_lse[pl.ds(i, 1), :] = peak + jnp.log(norm)
    mix = jnp.concatenate(mixes, axis=0)
    high = mix.astype(BF16)
    low = (mix - high.astype(F32)).astype(BF16)
    parts = got_out[...].reshape(rows, DH)
    own = jnp.dot(high, parts, preferred_element_type=F32) + jnp.dot(
        low, parts, preferred_element_type=F32
    )
    own_out[...] = own.astype(BF16).reshape(per, heads, DH)

    pl.semaphore_wait(far_sem, 2)
    b_slot = lax.div(z, seg) * (batch // per) + lax.rem(z, seg) * n_c + c
    b_rows = pl.ds(b_slot * per, per)
    all_out[b_slot] = own_out[...]
    all_lse[b_rows, :] = own_lse[...]
    b_count = 0
    order = sorted(range(-half + 1, half + 1), key=lambda d: -abs(d))
    for dz in order:
        for j in range(n_c):
            if dz == 0 and j == 0:
                continue
            for k, (src, dst) in enumerate(
                ((own_out, all_out.at[b_slot]), (own_lse, all_lse.at[b_rows, :]))
            ):
                copy = pltpu.make_async_remote_copy(
                    src_ref=src,
                    dst_ref=dst,
                    send_sem=b_send.at[k],
                    recv_sem=b_recv.at[k],
                    device_id={"seq": ring(dz), "sub": core(j)},
                    device_id_type=MESH,
                )
                copy.start()
            b_count += 1
    pl.semaphore_wait(side_sem.at[0], 2)
    for dx in (2, n_x - 2):
        pl.semaphore_signal(
            side_sem.at[1], inc=1, device_id={"head": lax.rem(x + dx, n_x)}, device_id_type=MESH
        )
    w_load.wait()
    wait_all(part_lse, a_count * per, a_send.at[1])
    wait_all(part_out, a_count, a_send.at[0])
    wait_all(all_lse, b_count * per, b_recv.at[1])
    wait_all(all_out, b_count, b_recv.at[0])

    levels = [all_lse[i * batch : (i + 1) * batch, :] for i in range(COPIES)]
    peak = functools.reduce(jnp.maximum, levels)
    weights = [jnp.exp(level - peak) for level in levels]
    inv = 1.0 / sum(weights)
    spot = lax.broadcasted_iota(jnp.int32, (batch, heads, rows), 0) * heads
    spot = spot + lax.broadcasted_iota(jnp.int32, (batch, heads, rows), 1)
    here = lax.broadcasted_iota(jnp.int32, (batch, heads, rows), 2) == spot
    blocks = []
    for weight in weights:
        expanded = jnp.broadcast_to((weight * inv)[:, None, :], (batch, heads, rows))
        blocks.append(jnp.where(here, expanded, 0.0).reshape(rows, rows))
    mix = jnp.concatenate(blocks, axis=1)
    high = mix.astype(BF16)
    low = (mix - high.astype(F32)).astype(BF16)
    parts = all_out[...].reshape(COPIES * rows, DH)
    att_rows[...] = jnp.dot(high, parts, preferred_element_type=F32) + jnp.dot(
        low, parts, preferred_element_type=F32
    )
    attention = jnp.concatenate(
        [att_rows[pl.ds(h, batch, stride=heads), :] for h in range(heads)], axis=1
    ).astype(BF16)
    projected = jnp.dot(attention, w_ref[...], preferred_element_type=F32)
    proj_mine[...] = projected.astype(BF16)
    proj_all[x] = proj_mine[...]

    pl.semaphore_wait(side_sem.at[1], 2)
    for dx in sorted(range(1, n_x), key=lambda d: -min(d, n_x - d)):
        copy = pltpu.make_async_remote_copy(
            src_ref=proj_mine,
            dst_ref=proj_all.at[x],
            send_sem=c_send,
            recv_sem=c_recv,
            device_id={"head": lax.rem(x + dx, n_x)},
            device_id_type=MESH,
        )
        copy.start()
    wait_all(all_lse, b_count * per, b_send.at[1])
    wait_all(all_out, b_count, b_send.at[0])
    wait_all(proj_all, n_x - 1, c_send)
    wait_all(proj_all, n_x - 1, c_recv)
    summed = proj_all[0].astype(F32)
    for i in range(1, n_x):
        summed = summed + proj_all[i].astype(F32)
    out_ref[...] = summed.astype(out_ref.dtype)


def on_device(sizes, queries, key_cache, value_cache, seq_lengths, slot_owner, slot_page, out_weight):
    n_z, n_x, n_c = sizes
    batch, heads = queries.shape[0], queries.shape[1] // DH
    slots = key_cache.shape[0]
    rows = batch * heads
    width = out_weight.shape[1]
    sources = n_z // COPIES * n_c
    per = batch // sources
    assert key_cache.shape[2] == DH and sources * per == batch and rows == DH
    hbm = pl.BlockSpec(memory_space=pltpu.HBM)
    dma = pltpu.SemaphoreType.DMA
    return pl.pallas_call(
        functools.partial(kernel, sizes),
        out_shape=pltpu.VMEM((batch, width), BF16),
        in_specs=[hbm] * 8,
        out_specs=pl.BlockSpec(memory_space=pltpu.VMEM),
        scratch_shapes=[
            pltpu.SMEM((batch,), jnp.int32),
            pltpu.SMEM((slots,), jnp.int32),
            pltpu.SMEM((slots,), jnp.int32),
            pltpu.VMEM((1, slots), jnp.int32),
            pltpu.VMEM(queries.shape, BF16),
            pltpu.VMEM(key_cache.shape, BF16),
            pltpu.VMEM(value_cache.shape, BF16),
            pltpu.VMEM(out_weight.shape, BF16),
            pltpu.VMEM((rows, DH), F32),
            pltpu.VMEM((batch, heads, DH), F32),
            pltpu.VMEM((slots * heads, PAGE), F32),
            pltpu.VMEM((slots * heads, PAGE), F32),
            pltpu.VMEM((rows, slots * heads), BF16),
            pltpu.VMEM((batch, heads, rows), F32),
            pltpu.VMEM((rows, rows), F32),
            pltpu.VMEM((batch // per, per, heads, DH), BF16),
            pltpu.VMEM((batch, rows), F32),
            pltpu.VMEM((sources, per, heads, DH), BF16),
            pltpu.VMEM((batch, rows), F32),
            pltpu.VMEM((per, heads, DH), BF16),
            pltpu.VMEM((per, rows), F32),
            pltpu.VMEM((COPIES * batch // per, per, heads, DH), BF16),
            pltpu.VMEM((COPIES * batch, rows), F32),
            pltpu.VMEM((rows, DH), F32),
            pltpu.VMEM((batch, width), BF16),
            pltpu.VMEM((n_x, batch, width), BF16),
            dma((5,)),
            dma,
            dma,
            dma,
            dma((2,)),
            dma((2,)),
            dma((2,)),
            dma((2,)),
            dma,
            dma,
            pltpu.SemaphoreType.REGULAR,
            pltpu.SemaphoreType.REGULAR((2,)),
        ],
        compiler_params=pltpu.CompilerParams(collective_id=0, has_side_effects=True),
        name="decode",
    )(
        seq_lengths,
        slot_owner,
        slot_page,
        slot_owner.reshape(1, slots),
        queries,
        key_cache,
        value_cache,
        out_weight,
    )


def solution(mesh):
    sizes = (mesh.shape["seq"], mesh.shape["head"], mesh.shape["sub"])
    in_specs = (
        P("rep", "head"),
        P(("rep", "seq", "sub"), None, "head"),
        P(("rep", "seq", "sub"), None, "head"),
        P("rep"),
        P(("rep", "seq", "sub")),
        P(("rep", "seq", "sub")),
        P("head", ("seq", "sub")),
    )
    out_specs = P("rep", ("seq", "sub"))
    return jax.shard_map(
        functools.partial(on_device, sizes),
        mesh=mesh,
        in_specs=in_specs,
        out_specs=out_specs,
        check_vma=False,
    )
```

time: 66.1 us -> 65.1 us (0.985)
  Pallas kernels: 65.4 us -> 64.4 us
    pallas_call x1, Pallas kernels: 65.4 us -> 64.4 us  [on_device(): pl.pallas_call(functools.partial(kernel, sizes), out_shape=pltpu.VMEM((ba...]
where the time goes in v3:
time: 65.1 us; the launch traced here: 65 us
  Pallas kernels  64.4 us (99%)
    pallas_call x1, Pallas kernels, on_device(): pl.pallas_call(functools.partial(kernel, sizes), out_shape=pltpu.VMEM((ba...  64.4 us

profile of v3, /device:TPU:65, one launch (start us, length us, event | category | flops | bytes accessed | tf_op | source)
XLA Modules:
  0.0 65.0 jit_solution(8155394571838853466)
XLA Ops:
  0.0 64.4 %decode.1 = bf16[16,256]{1,0:T(8,128)(2,1)S(1)} custom-call(s32[16]{0:T(128)} %lengths_hbm.1, s32[64]{0:T(128)} %owners_hbm.1, s32[64]{0:T(128)} %numbers_hbm.1, s32[1,64]{1,0:T(1,128)} %bitcast.1, bf16[16,1024]{1,0:T(8,128)(2,1)} %q_hbm.1, bf16[64,128,128]{2,1,0:T(8,128)(2,1)} %k_hbm.1, bf16[64,128,128]{2,1,0:T(8,128)(2,1)} %v_hbm.1, bf16[1024,256]{1,0:T(8,128)(2,1)} %w_hbm.1), custom_call_target="tpu_custom_call" | custom-call | tf_op jit(solution)/shard_map/decode/pallas_call | solution.py:380
  64.4 0.6 copy.9

commit v4 on v3

v4 whole, which is shorter than its diff:
```python
import functools

import jax
import jax.numpy as jnp
from jax import lax
from jax.experimental import pallas as pl
from jax.experimental.pallas import tpu as pltpu
from jax.sharding import PartitionSpec as P

DH = 128
PAGE = 128
NEG = -1e30
COPIES = 2
F32 = jnp.float32
BF16 = jnp.bfloat16
MESH = pl.DeviceIdType.MESH


def kernel(
    sizes,
    lengths_hbm,
    owners_hbm,
    numbers_hbm,
    owner_row_hbm,
    q_hbm,
    k_hbm,
    v_hbm,
    w_hbm,
    out_ref,
    lengths,
    owners,
    numbers,
    owner_row,
    q_ref,
    k_ref,
    v_ref,
    w_ref,
    q_rows,
    q_seq,
    peaks,
    masses,
    hits,
    seq_lse,
    lse_diag,
    part_out,
    part_lse,
    got_out,
    got_lse,
    own_out,
    own_lse,
    all_out,
    all_lse,
    att_rows,
    proj_mine,
    proj_all,
    small_sem,
    k_sem,
    v_sem,
    w_sem,
    w_pass,
    a_send,
    a_recv,
    b_send,
    b_recv,
    c_send,
    c_recv,
    far_sem,
    side_sem,
):
    n_z, n_x, n_c = sizes
    batch, heads, slots = lengths.shape[0], q_ref.shape[1] // DH, owners.shape[0]
    half = n_z // 2
    near = half // 2
    seg = n_z // COPIES
    per = batch // seg
    top = n_c - 1
    sources = seg * n_c
    z, x, c = lax.axis_index("seq"), lax.axis_index("head"), lax.axis_index("sub")
    rows = batch * heads

    def ring(offset):
        return lax.rem(z + offset + n_z, n_z)

    small = [
        pltpu.make_async_copy(src, dst, small_sem.at[i])
        for i, (src, dst) in enumerate(
            (
                (owners_hbm, owners),
                (lengths_hbm, lengths),
                (numbers_hbm, numbers),
                (owner_row_hbm, owner_row),
                (q_hbm, q_ref),
            )
        )
    ]
    k_load = pltpu.make_async_copy(k_hbm, k_ref, k_sem)
    v_load = pltpu.make_async_copy(v_hbm, v_ref, v_sem)
    w_load = pltpu.make_async_copy(w_hbm, w_ref.at[top], w_sem)
    for copy in small + [k_load, v_load]:
        copy.start()

    def wait_all(ref, count, sem):
        span = ref.at[pl.ds(0, count)]
        pltpu.make_async_copy(span, span, sem).wait()

    barrier = pltpu.get_barrier_semaphore()

    def greet(**where):
        pl.semaphore_signal(barrier, inc=1, device_id=where, device_id_type=MESH)

    @pl.when(c == top)
    def _():
        for dz in sorted(range(-near, near + 1), key=lambda d: -abs(d)):
            for core in range(n_c):
                if dz or core != top:
                    greet(seq=ring(dz), sub=core)
        for dx in (1, n_x - 1):
            greet(head=lax.rem(x + dx, n_x), sub=top)
        w_load.start()

    @pl.when(c != top)
    def _():
        for dx in (0, 1, n_x - 1):
            greet(head=lax.rem(x + dx, n_x), sub=top)

    greeted_top = 2 * near + (n_c - 1) + 2 * n_c
    greeted_other = 2 * near + 1

    for copy in small:
        copy.wait()

    lane = lax.broadcasted_iota(jnp.int32, (heads, rows), 1)
    sub = lax.broadcasted_iota(jnp.int32, (heads, rows), 0)
    diag = lane - sub

    for h in range(heads):
        q_rows[pl.ds(h, batch, stride=heads), :] = q_ref[:, h * DH : (h + 1) * DH].astype(F32)
    q_seq[...] = q_rows[...].reshape(batch, heads, DH)

    hit = (lax.broadcasted_iota(jnp.int32, (batch, slots), 0) == owner_row[...]).astype(BF16)
    spread_rows = lax.broadcasted_iota(jnp.int32, (slots, slots * heads), 0)
    spread_cols = lax.broadcasted_iota(jnp.int32, (slots, slots * heads), 1)
    spread = (spread_cols // heads == spread_rows).astype(BF16)
    wide = jnp.dot(hit, spread, preferred_element_type=F32)
    wide = jnp.broadcast_to(wide[:, None, :], (batch, heads, slots * heads))
    w_sub = lax.broadcasted_iota(jnp.int32, (batch, heads, slots * heads), 1)
    w_lane = lax.broadcasted_iota(jnp.int32, (batch, heads, slots * heads), 2)
    hits[...] = jnp.where(w_lane % heads == w_sub, wide, 0.0).reshape(rows, slots * heads).astype(BF16)

    scale = 1.0 / (float(DH) ** 0.5)
    pair_sub = lax.broadcasted_iota(jnp.int32, (2 * heads, PAGE), 0)
    pair_lane = lax.broadcasted_iota(jnp.int32, (2 * heads, PAGE), 1)
    first = pair_sub < heads

    probs = []
    peak_diag = jnp.full((heads, rows), NEG, F32)
    k_load.wait()
    for pair in range(slots // 2):
        a, b = 2 * pair, 2 * pair + 1
        own_a, own_b = owners[a], owners[b]
        q_pair = jnp.concatenate(
            [
                q_seq[own_a],
                q_seq[own_b],
            ],
            axis=0,
        ).astype(BF16)
        keys = k_ref[a : b + 1].reshape(2 * PAGE, DH)
        both = lax.dot_general(
            q_pair, keys, (((1,), (1,)), ((), ())), preferred_element_type=F32
        )
        scores = jnp.concatenate([both[:heads, :PAGE], both[heads:, PAGE:]], axis=0) * scale
        live_a = jnp.clip(lengths[own_a] - numbers[a] * PAGE, 0, PAGE)
        live_b = jnp.clip(lengths[own_b] - numbers[b] * PAGE, 0, PAGE)
        scores = jnp.where(pair_lane < jnp.where(first, live_a, live_b), scores, NEG)
        peak = jnp.max(scores, axis=1, keepdims=True)
        prob = jnp.exp(scores - peak).astype(BF16)
        mass = jnp.sum(prob.astype(F32), axis=1, keepdims=True)
        peak = jnp.broadcast_to(peak, (2 * heads, PAGE))
        mass = jnp.broadcast_to(mass, (2 * heads, PAGE))
        peaks[pl.ds(a * heads, 2 * heads), :] = peak
        masses[pl.ds(a * heads, 2 * heads), :] = mass
        probs.append(prob)
        peak_diag = jnp.maximum(peak_diag, jnp.where(diag == own_a * heads, peak[:heads], NEG))
        peak_diag = jnp.maximum(peak_diag, jnp.where(diag == own_b * heads, peak[heads:], NEG))

    v_load.wait()

    def by_sequence(row_values):
        for b in range(batch):
            mine = jnp.max(
                jnp.where(lane // heads == b, row_values, 2 * NEG), axis=1, keepdims=True
            )
            seq_lse[b] = jnp.broadcast_to(mine, (heads, rows))

    by_sequence(peak_diag)
    total = jnp.zeros((heads, rows), F32)
    for s in range(slots):
        span = pl.ds(s * heads, heads)
        factor = jnp.exp(peaks[span, :] - seq_lse[owners[s]])
        total = total + jnp.where(diag == owners[s] * heads, factor * masses[span, :], 0.0)
    lse = jnp.where(total > 0.0, peak_diag + jnp.log(jnp.where(total > 0.0, total, 1.0)), NEG)
    by_sequence(lse)

    for b in range(batch):
        lse_diag[pl.ds(b * heads, heads), :] = jnp.where(lane % heads == sub, seq_lse[b], 0.0)
    tiled = lse_diag[pl.ds(0, batch, stride=heads), :]
    for h in range(1, heads):
        tiled = tiled + lse_diag[pl.ds(h, batch, stride=heads), :]
    part_lse[...] = tiled

    high, low = [], []
    for pair in range(slots // 2):
        a, b = 2 * pair, 2 * pair + 1
        prob = probs[pair]
        block = jnp.concatenate(
            [
                jnp.where(first, prob, jnp.zeros_like(prob)),
                jnp.where(first, jnp.zeros_like(prob), prob),
            ],
            axis=1,
        )
        values = v_ref[a : b + 1].reshape(2 * PAGE, DH)
        page_out = jnp.dot(block, values, preferred_element_type=F32)
        span = pl.ds(a * heads, 2 * heads)
        level = jnp.concatenate([seq_lse[owners[a]], seq_lse[owners[b]]], axis=0)
        factor = jnp.exp(peaks[span, :] - level)
        page_out = page_out * factor
        high.append(page_out.astype(BF16))
        low.append((page_out - high[-1].astype(F32)).astype(BF16))
    hit = hits[...]
    mine = jnp.dot(hit, jnp.concatenate(high, axis=0), preferred_element_type=F32)
    mine = mine + jnp.dot(hit, jnp.concatenate(low, axis=0), preferred_element_type=F32)
    part_out[...] = mine.astype(BF16).reshape(seg, per, heads, DH)

    def send_parts(core):
        sent = 0
        for dz in sorted(range(-(seg // 2), seg // 2), key=lambda d: -abs(d)):
            target = lax.rem(ring(dz), seg)
            slot = (seg // 2 - 1 - dz) * n_c + core
            src_rows, dst_rows = pl.ds(target * per, per), pl.ds(slot * per, per)
            if dz == 0 and core == top:
                got_out[slot] = part_out[target]
                got_lse[dst_rows, :] = part_lse[src_rows, :]
                continue
            for k, (src, dst) in enumerate(
                (
                    (part_out.at[target], got_out.at[slot]),
                    (part_lse.at[src_rows, :], got_lse.at[dst_rows, :]),
                )
            ):
                pltpu.make_async_remote_copy(
                    src_ref=src,
                    dst_ref=dst,
                    send_sem=a_send.at[k],
                    recv_sem=a_recv.at[k],
                    device_id={"seq": ring(dz), "sub": top},
                    device_id_type=MESH,
                ).start()
            sent += 1
        return sent

    def other_core():
        pl.semaphore_wait(barrier, greeted_other)
        sent = send_parts(0)
        weights = pltpu.make_async_remote_copy(
            src_ref=w_hbm,
            dst_ref=w_ref.at[0],
            send_sem=w_pass.at[0],
            recv_sem=w_pass.at[1],
            device_id={"sub": top},
            device_id_type=MESH,
        )
        weights.start()
        wait_all(part_lse, sent * per, a_send.at[1])
        wait_all(part_out, sent, a_send.at[0])
        weights.wait_send()
        wait_all(proj_all, n_x, c_recv)

    def top_core():
        pl.semaphore_wait(barrier, greeted_top)
        sent = send_parts(top)
        for dz in (-near, near):
            pl.semaphore_signal(far_sem, inc=1, device_id={"seq": ring(dz)}, device_id_type=MESH)
        for dx in (1, n_x - 1):
            pl.semaphore_signal(
                side_sem.at[0], inc=1, device_id={"head": lax.rem(x + dx, n_x)}, device_id_type=MESH
            )
        wait_all(got_lse, (sources - 1) * per, a_recv.at[1])
        wait_all(got_out, sources - 1, a_recv.at[0])

        wide_rows = rows * n_c
        s_sub = lax.broadcasted_iota(jnp.int32, (sources, wide_rows), 0)
        s_lane = lax.broadcasted_iota(jnp.int32, (sources, wide_rows), 1)
        m_lane = lax.broadcasted_iota(jnp.int32, (heads, wide_rows), 1)
        m_sub = lax.broadcasted_iota(jnp.int32, (heads, wide_rows), 0)
        mixes = []
        for i in range(per):
            levels = got_lse[pl.ds(i, sources, stride=per), :]
            peak = jnp.max(levels, axis=0, keepdims=True)
            weight = jnp.exp(levels - peak)
            norm = jnp.sum(weight, axis=0, keepdims=True)
            weight = jnp.concatenate([weight / norm] * n_c, axis=1)
            flat = jnp.sum(
                jnp.where(s_lane // heads == s_sub * per + i, weight, 0.0), axis=0, keepdims=True
            )
            mixes.append(jnp.where(m_lane % heads == m_sub, jnp.broadcast_to(flat, (heads, wide_rows)), 0.0))
            own_lse[pl.ds(i, 1), :] = peak + jnp.log(norm)
        mix = jnp.concatenate(mixes, axis=0)
        high = mix.astype(BF16)
        low = (mix - high.astype(F32)).astype(BF16)
        parts = got_out[...].reshape(wide_rows, DH)
        own = jnp.dot(high, parts, preferred_element_type=F32) + jnp.dot(
            low, parts, preferred_element_type=F32
        )
        own_out[...] = own.astype(BF16).reshape(per, heads, DH)

        pl.semaphore_wait(far_sem, 2)
        b_rows = pl.ds(z * per, per)
        all_out[z] = own_out[...]
        all_lse[b_rows, :] = own_lse[...]
        for dz in sorted(range(-half + 1, half + 1), key=lambda d: -abs(d)):
            if dz == 0:
                continue
            for k, (src, dst) in enumerate(
                ((own_out, all_out.at[z]), (own_lse, all_lse.at[b_rows, :]))
            ):
                pltpu.make_async_remote_copy(
                    src_ref=src,
                    dst_ref=dst,
                    send_sem=b_send.at[k],
                    recv_sem=b_recv.at[k],
                    device_id={"seq": ring(dz)},
                    device_id_type=MESH,
                ).start()
        pl.semaphore_wait(side_sem.at[0], 2)
        for dx in (2, n_x - 2):
            pl.semaphore_signal(
                side_sem.at[1], inc=1, device_id={"head": lax.rem(x + dx, n_x)}, device_id_type=MESH
            )
        w_load.wait()
        pltpu.make_async_copy(w_ref.at[0], w_ref.at[0], w_pass.at[1]).wait()
        wait_all(part_lse, sent * per, a_send.at[1])
        wait_all(part_out, sent, a_send.at[0])
        wait_all(all_lse, (n_z - 1) * per, b_recv.at[1])
        wait_all(all_out, n_z - 1, b_recv.at[0])

        levels = [all_lse[i * batch : (i + 1) * batch, :] for i in range(COPIES)]
        peak = functools.reduce(jnp.maximum, levels)
        weights = [jnp.exp(level - peak) for level in levels]
        inv = 1.0 / sum(weights)
        spot = lax.broadcasted_iota(jnp.int32, (batch, heads, rows), 0) * heads
        spot = spot + lax.broadcasted_iota(jnp.int32, (batch, heads, rows), 1)
        here = lax.broadcasted_iota(jnp.int32, (batch, heads, rows), 2) == spot
        blocks = []
        for weight in weights:
            expanded = jnp.broadcast_to((weight * inv)[:, None, :], (batch, heads, rows))
            blocks.append(jnp.where(here, expanded, 0.0).reshape(rows, rows))
        mix = jnp.concatenate(blocks, axis=1)
        high = mix.astype(BF16)
        low = (mix - high.astype(F32)).astype(BF16)
        parts = all_out[...].reshape(COPIES * rows, DH)
        att_rows[...] = jnp.dot(high, parts, preferred_element_type=F32) + jnp.dot(
            low, parts, preferred_element_type=F32
        )
        attention = jnp.concatenate(
            [att_rows[pl.ds(h, batch, stride=heads), :] for h in range(heads)], axis=1
        ).astype(BF16)
        for core in range(n_c):
            proj_mine[core] = jnp.dot(
                attention, w_ref[core], preferred_element_type=F32
            ).astype(BF16)
        proj_all[x] = proj_mine[top]

        pl.semaphore_wait(side_sem.at[1], 2)
        for dx in sorted(range(n_x), key=lambda d: -min(d, n_x - d)):
            for core in range(n_c):
                if dx == 0 and core == top:
                    continue
                pltpu.make_async_remote_copy(
                    src_ref=proj_mine.at[core],
                    dst_ref=proj_all.at[x],
                    send_sem=c_send.at[core],
                    recv_sem=c_recv,
                    device_id={"head": lax.rem(x + dx, n_x), "sub": core},
                    device_id_type=MESH,
                ).start()
        wait_all(all_lse, (n_z - 1) * per, b_send.at[1])
        wait_all(all_out, n_z - 1, b_send.at[0])
        wait_all(proj_all, n_x, c_send.at[0])
        wait_all(proj_all, n_x - 1, c_send.at[top])
        wait_all(proj_all, n_x - 1, c_recv)

    pl.when(c != top)(other_core)
    pl.when(c == top)(top_core)
    summed = proj_all[0].astype(F32)
    for i in range(1, n_x):
        summed = summed + proj_all[i].astype(F32)
    out_ref[...] = summed.astype(out_ref.dtype)


def on_device(sizes, queries, key_cache, value_cache, seq_lengths, slot_owner, slot_page, out_weight):
    n_z, n_x, n_c = sizes
    batch, heads = queries.shape[0], queries.shape[1] // DH
    slots = key_cache.shape[0]
    rows = batch * heads
    width = out_weight.shape[1]
    sources = n_z // COPIES * n_c
    per = batch // (n_z // COPIES)
    assert key_cache.shape[2] == DH and rows == DH and n_c == 2
    hbm = pl.BlockSpec(memory_space=pltpu.HBM)
    dma = pltpu.SemaphoreType.DMA
    return pl.pallas_call(
        functools.partial(kernel, sizes),
        out_shape=pltpu.VMEM((batch, width), BF16),
        in_specs=[hbm] * 8,
        out_specs=pl.BlockSpec(memory_space=pltpu.VMEM),
        scratch_shapes=[
            pltpu.SMEM((batch,), jnp.int32),
            pltpu.SMEM((slots,), jnp.int32),
            pltpu.SMEM((slots,), jnp.int32),
            pltpu.VMEM((1, slots), jnp.int32),
            pltpu.VMEM(queries.shape, BF16),
            pltpu.VMEM(key_cache.shape, BF16),
            pltpu.VMEM(value_cache.shape, BF16),
            pltpu.VMEM((n_c, *out_weight.shape), BF16),
            pltpu.VMEM((rows, DH), F32),
            pltpu.VMEM((batch, heads, DH), F32),
            pltpu.VMEM((slots * heads, PAGE), F32),
            pltpu.VMEM((slots * heads, PAGE), F32),
            pltpu.VMEM((rows, slots * heads), BF16),
            pltpu.VMEM((batch, heads, rows), F32),
            pltpu.VMEM((rows, rows), F32),
            pltpu.VMEM((batch // per, per, heads, DH), BF16),
            pltpu.VMEM((batch, rows), F32),
            pltpu.VMEM((sources, per, heads, DH), BF16),
            pltpu.VMEM((sources * per, rows), F32),
            pltpu.VMEM((per, heads, DH), BF16),
            pltpu.VMEM((per, rows), F32),
            pltpu.VMEM((n_z, per, heads, DH), BF16),
            pltpu.VMEM((n_z * per, rows), F32),
            pltpu.VMEM((rows, DH), F32),
            pltpu.VMEM((n_c, batch, width), BF16),
            pltpu.VMEM((n_x, batch, width), BF16),
            dma((5,)),
            dma,
            dma,
            dma,
            dma((2,)),
            dma((2,)),
            dma((2,)),
            dma((2,)),
            dma((2,)),
            dma((n_c,)),
            dma,
            pltpu.SemaphoreType.REGULAR,
            pltpu.SemaphoreType.REGULAR((2,)),
        ],
        compiler_params=pltpu.CompilerParams(collective_id=0, has_side_effects=True),
        name="decode",
    )(
        seq_lengths,
        slot_owner,
        slot_page,
        slot_owner.reshape(1, slots),
        queries,
        key_cache,
        value_cache,
        out_weight,
    )


def solution(mesh):
    sizes = (mesh.shape["seq"], mesh.shape["head"], mesh.shape["sub"])
    in_specs = (
        P("rep", "head"),
        P(("rep", "seq", "sub"), None, "head"),
        P(("rep", "seq", "sub"), None, "head"),
        P("rep"),
        P(("rep", "seq", "sub")),
        P(("rep", "seq", "sub")),
        P("head", ("seq", "sub")),
    )
    out_specs = P("rep", ("seq", "sub"))
    return jax.shard_map(
        functools.partial(on_device, sizes),
        mesh=mesh,
        in_specs=in_specs,
        out_specs=out_specs,
        check_vma=False,
    )
```

time: 65.1 us -> 63.5 us (0.975)
  Pallas kernels: 64.4 us -> 62.8 us
    pallas_call x1, Pallas kernels: 64.4 us -> 62.8 us  [on_device(): pl.pallas_call(functools.partial(kernel, sizes), out_shape=pltpu.VMEM((ba...]
where the time goes in v4:
time: 63.5 us; the launch traced here: 63.4 us
  Pallas kernels  62.8 us (99%)
    pallas_call x1, Pallas kernels, on_device(): pl.pallas_call(functools.partial(kernel, sizes), out_shape=pltpu.VMEM((ba...  62.8 us

profile of v4, /device:TPU:65, one launch (start us, length us, event | category | flops | bytes accessed | tf_op | source)
XLA Modules:
  0.0 63.4 jit_solution(8982286159810966849)
XLA Ops:
  0.0 62.8 %decode.1 = bf16[16,256]{1,0:T(8,128)(2,1)S(1)} custom-call(s32[16]{0:T(128)} %lengths_hbm.1, s32[64]{0:T(128)} %owners_hbm.1, s32[64]{0:T(128)} %numbers_hbm.1, s32[1,64]{1,0:T(1,128)} %bitcast.1, bf16[16,1024]{1,0:T(8,128)(2,1)} %q_hbm.1, bf16[64,128,128]{2,1,0:T(8,128)(2,1)} %k_hbm.1, bf16[64,128,128]{2,1,0:T(8,128)(2,1)} %v_hbm.1, bf16[1024,256]{1,0:T(8,128)(2,1)} %w_hbm.1), custom_call_target="tpu_custom_call" | custom-call | tf_op jit(solution)/shard_map/decode/pallas_call | solution.py:413
  62.8 0.6 copy.9

commit v5 on v4

--- a/solution.py
+++ b/solution.py
@@ -10,7 +10,7 @@
 DH = 128
 PAGE = 128
 NEG = -1e30
-COPIES = 2
+COPIES = 4
 F32 = jnp.float32
 BF16 = jnp.bfloat16
 MESH = pl.DeviceIdType.MESH
@@ -116,7 +116,6 @@
                     greet(seq=ring(dz), sub=core)
         for dx in (1, n_x - 1):
             greet(head=lax.rem(x + dx, n_x), sub=top)
-        w_load.start()
 
     @pl.when(c != top)
     def _():
@@ -279,9 +278,10 @@
 
     def top_core():
         pl.semaphore_wait(barrier, greeted_top)
-        sent = send_parts(top)
         for dz in (-near, near):
             pl.semaphore_signal(far_sem, inc=1, device_id={"seq": ring(dz)}, device_id_type=MESH)
+        sent = send_parts(top)
+        w_load.start()
         for dx in (1, n_x - 1):
             pl.semaphore_signal(
                 side_sem.at[0], inc=1, device_id={"head": lax.rem(x + dx, n_x)}, device_id_type=MESH

time: 63.5 us -> 63.8 us (level)
  no operation moved by 1% of the time
where the time goes in v5:
time: 63.8 us; the launch traced here: 63.7 us
  Pallas kernels  63.1 us (99%)
    pallas_call x1, Pallas kernels, on_device(): pl.pallas_call(functools.partial(kernel, sizes), out_shape=pltpu.VMEM((ba...  63.1 us

profile of v5, /device:TPU:65, one launch (start us, length us, event | category | flops | bytes accessed | tf_op | source)
XLA Modules:
  0.0 63.7 jit_solution(12240086175125652403)
XLA Ops:
  0.0 63.1 %decode.1 = bf16[16,256]{1,0:T(8,128)(2,1)S(1)} custom-call(s32[16]{0:T(128)} %lengths_hbm.1, s32[64]{0:T(128)} %owners_hbm.1, s32[64]{0:T(128)} %numbers_hbm.1, s32[1,64]{1,0:T(1,128)} %bitcast.1, bf16[16,1024]{1,0:T(8,128)(2,1)} %q_hbm.1, bf16[64,128,128]{2,1,0:T(8,128)(2,1)} %k_hbm.1, bf16[64,128,128]{2,1,0:T(8,128)(2,1)} %v_hbm.1, bf16[1024,256]{1,0:T(8,128)(2,1)} %w_hbm.1), custom_call_target="tpu_custom_call" | custom-call | tf_op jit(solution)/shard_map/decode/pallas_call | solution.py:413
  63.1 0.6 copy.9

commit v6 on v5

--- a/solution.py
+++ b/solution.py
@@ -40,6 +40,7 @@
     peaks,
     masses,
     hits,
+    seq_peak,
     seq_lse,
     lse_diag,
     part_out,
@@ -183,23 +184,41 @@
         peak_diag = jnp.maximum(peak_diag, jnp.where(diag == own_a * heads, peak[:heads], NEG))
         peak_diag = jnp.maximum(peak_diag, jnp.where(diag == own_b * heads, peak[heads:], NEG))
 
+
+    @pl.when(c == top)
+    def _():
+        pl.semaphore_wait(barrier, greeted_top)
+        for dz in (-near, near):
+            pl.semaphore_signal(far_sem, inc=1, device_id={"seq": ring(dz)}, device_id_type=MESH)
+        for dx in (1, n_x - 1):
+            pl.semaphore_signal(
+                side_sem.at[0], inc=1, device_id={"head": lax.rem(x + dx, n_x)}, device_id_type=MESH
+            )
+
+    @pl.when(c != top)
+    def _():
+        pl.semaphore_wait(barrier, greeted_other)
+
     v_load.wait()
 
-    def by_sequence(row_values):
+    def by_sequence(row_values, ref):
         for b in range(batch):
             mine = jnp.max(
                 jnp.where(lane // heads == b, row_values, 2 * NEG), axis=1, keepdims=True
             )
-            seq_lse[b] = jnp.broadcast_to(mine, (heads, rows))
-
-    by_sequence(peak_diag)
+            ref[b] = jnp.broadcast_to(mine, (heads, rows))
+
+    by_sequence(peak_diag, seq_peak)
     total = jnp.zeros((heads, rows), F32)
+    factors = []
     for s in range(slots):
         span = pl.ds(s * heads, heads)
-        factor = jnp.exp(peaks[span, :] - seq_lse[owners[s]])
-        total = total + jnp.where(diag == owners[s] * heads, factor * masses[span, :], 0.0)
-    lse = jnp.where(total > 0.0, peak_diag + jnp.log(jnp.where(total > 0.0, total, 1.0)), NEG)
-    by_sequence(lse)
+        factors.append(jnp.exp(peaks[span, :] - seq_peak[owners[s]]))
+        total = total + jnp.where(diag == owners[s] * heads, factors[s] * masses[span, :], 0.0)
+    lse = jnp.where(
+        total > 0.0, peak_diag + jnp.log(jnp.where(total > 0.0, total, 1.0)), NEG
+    )
+    by_sequence(lse, seq_lse)
 
     for b in range(batch):
         lse_diag[pl.ds(b * heads, heads), :] = jnp.where(lane % heads == sub, seq_lse[b], 0.0)
@@ -221,15 +240,13 @@
         )
         values = v_ref[a : b + 1].reshape(2 * PAGE, DH)
         page_out = jnp.dot(block, values, preferred_element_type=F32)
-        span = pl.ds(a * heads, 2 * heads)
-        level = jnp.concatenate([seq_lse[owners[a]], seq_lse[owners[b]]], axis=0)
-        factor = jnp.exp(peaks[span, :] - level)
-        page_out = page_out * factor
+        page_out = page_out * jnp.concatenate([factors[a], factors[b]], axis=0)
         high.append(page_out.astype(BF16))
         low.append((page_out - high[-1].astype(F32)).astype(BF16))
     hit = hits[...]
     mine = jnp.dot(hit, jnp.concatenate(high, axis=0), preferred_element_type=F32)
     mine = mine + jnp.dot(hit, jnp.concatenate(low, axis=0), preferred_element_type=F32)
+    mine = mine * jnp.exp(seq_peak[...] - seq_lse[...]).reshape(rows, rows)
     part_out[...] = mine.astype(BF16).reshape(seg, per, heads, DH)
 
     def send_parts(core):
@@ -260,7 +277,6 @@
         return sent
 
     def other_core():
-        pl.semaphore_wait(barrier, greeted_other)
         sent = send_parts(0)
         weights = pltpu.make_async_remote_copy(
             src_ref=w_hbm,
@@ -277,15 +293,8 @@
         wait_all(proj_all, n_x, c_recv)
 
     def top_core():
-        pl.semaphore_wait(barrier, greeted_top)
-        for dz in (-near, near):
-            pl.semaphore_signal(far_sem, inc=1, device_id={"seq": ring(dz)}, device_id_type=MESH)
         sent = send_parts(top)
         w_load.start()
-        for dx in (1, n_x - 1):
-            pl.semaphore_signal(
-                side_sem.at[0], inc=1, device_id={"head": lax.rem(x + dx, n_x)}, device_id_type=MESH
-            )
         wait_all(got_lse, (sources - 1) * per, a_recv.at[1])
         wait_all(got_out, sources - 1, a_recv.at[0])
 
@@ -429,6 +438,7 @@
             pltpu.VMEM((slots * heads, PAGE), F32),
             pltpu.VMEM((slots * heads, PAGE), F32),
             pltpu.VMEM((rows, slots * heads), BF16),
+            pltpu.VMEM((batch, heads, rows), F32),
             pltpu.VMEM((batch, heads, rows), F32),
             pltpu.VMEM((rows, rows), F32),
             pltpu.VMEM((batch // per, per, heads, DH), BF16),

time: 63.8 us -> 63.3 us (level)
  no operation moved by 1% of the time
where the time goes in v6:
time: 63.3 us; the launch traced here: 63.2 us
  Pallas kernels  62.6 us (99%)
    pallas_call x1, Pallas kernels, on_device(): pl.pallas_call(functools.partial(kernel, sizes), out_shape=pltpu.VMEM((ba...  62.6 us

profile of v6, /device:TPU:65, one launch (start us, length us, event | category | flops | bytes accessed | tf_op | source)
XLA Modules:
  0.0 63.2 jit_solution(3289733859940338906)
XLA Ops:
  0.0 62.6 %decode.1 = bf16[16,256]{1,0:T(8,128)(2,1)S(1)} custom-call(s32[16]{0:T(128)} %lengths_hbm.1, s32[64]{0:T(128)} %owners_hbm.1, s32[64]{0:T(128)} %numbers_hbm.1, s32[1,64]{1,0:T(1,128)} %bitcast.1, bf16[16,1024]{1,0:T(8,128)(2,1)} %q_hbm.1, bf16[64,128,128]{2,1,0:T(8,128)(2,1)} %k_hbm.1, bf16[64,128,128]{2,1,0:T(8,128)(2,1)} %v_hbm.1, bf16[1024,256]{1,0:T(8,128)(2,1)} %w_hbm.1), custom_call_target="tpu_custom_call" | custom-call | tf_op jit(solution)/shard_map/decode/pallas_call | solution.py:422
  62.6 0.6 copy.9

commit v7 on v6

--- a/solution.py
+++ b/solution.py
@@ -319,9 +319,10 @@
         high = mix.astype(BF16)
         low = (mix - high.astype(F32)).astype(BF16)
         parts = got_out[...].reshape(wide_rows, DH)
-        own = jnp.dot(high, parts, preferred_element_type=F32) + jnp.dot(
-            low, parts, preferred_element_type=F32
+        both = jnp.dot(
+            jnp.concatenate([high, low], axis=0), parts, preferred_element_type=F32
         )
+        own = both[: per * heads] + both[per * heads :]
         own_out[...] = own.astype(BF16).reshape(per, heads, DH)
 
         pl.semaphore_wait(far_sem, 2)
@@ -369,9 +370,10 @@
         high = mix.astype(BF16)
         low = (mix - high.astype(F32)).astype(BF16)
         parts = all_out[...].reshape(COPIES * rows, DH)
-        att_rows[...] = jnp.dot(high, parts, preferred_element_type=F32) + jnp.dot(
-            low, parts, preferred_element_type=F32
+        both = jnp.dot(
+            jnp.concatenate([high, low], axis=0), parts, preferred_element_type=F32
         )
+        att_rows[...] = both[:rows] + both[rows:]
         attention = jnp.concatenate(
             [att_rows[pl.ds(h, batch, stride=heads), :] for h in range(heads)], axis=1
         ).astype(BF16)

time: 63.3 us -> 63.3 us (level)
  no operation moved by 1% of the time
where the time goes in v7:
time: 63.3 us; the launch traced here: 63.2 us
  Pallas kernels  62.6 us (99%)
    pallas_call x1, Pallas kernels, on_device(): pl.pallas_call(functools.partial(kernel, sizes), out_shape=pltpu.VMEM((ba...  62.6 us

profile of v7, /device:TPU:65, one launch (start us, length us, event | category | flops | bytes accessed | tf_op | source)
XLA Modules:
  0.0 63.2 jit_solution(14542742142884850709)
XLA Ops:
  0.0 62.6 %decode.1 = bf16[16,256]{1,0:T(8,128)(2,1)S(1)} custom-call(s32[16]{0:T(128)} %lengths_hbm.1, s32[64]{0:T(128)} %owners_hbm.1, s32[64]{0:T(128)} %numbers_hbm.1, s32[1,64]{1,0:T(1,128)} %bitcast.1, bf16[16,1024]{1,0:T(8,128)(2,1)} %q_hbm.1, bf16[64,128,128]{2,1,0:T(8,128)(2,1)} %k_hbm.1, bf16[64,128,128]{2,1,0:T(8,128)(2,1)} %v_hbm.1, bf16[1024,256]{1,0:T(8,128)(2,1)} %w_hbm.1), custom_call_target="tpu_custom_call" | custom-call | tf_op jit(solution)/shard_map/decode/pallas_call | solution.py:424
  62.6 0.6 copy.9
